TPU v7x, 8 devices: a whole 2x2x1 slice. The times are simulated.
8 devices in a mesh: dep: 2 (over z, y), col: 2 (over x), row: 2 (over core).
Axes of the slice: x: 2, y: 2, z: 1, core: 2. Of those that a mesh axis runs over, the one named last changes fastest.
Arguments:
- x_tok: bfloat16 [16384, 1024], P(('dep', 'row'), 'col')
- w_up: bfloat16 [1024, 4096], P('row', 'col')
- w_down: bfloat16 [4096, 1024], P('row', 'col')
- grad_out: bfloat16 [16384, 1024], P(('dep', 'row'), 'col')
Outputs:
- output 1: bfloat16 [16384, 1024], P(('dep', 'row'), 'col')
- output 2: bfloat16 [16384, 1024], P(('dep', 'row'), 'col')
- output 3: float32 [1024, 4096], P(('row', 'dep'), 'col')
- output 4: float32 [4096, 1024], P(('row', 'dep'), 'col')
All inputs are finite; a program needn't handle non-finite values.
Results may differ from a plain program's by a relative error of at most 0.001.
Values are sent between devices in bfloat16 or wider.
A program may use at most 1 GiB of HBM per device.

v0:
```python
import jax
import jax.numpy as jnp
from jax import lax
from jax.sharding import PartitionSpec as P, NamedSharding

GELU_COEF = 0.7978845608028654
CUBIC_COEF = 0.044715


def gelu_fwd(pre_act):
    inner = GELU_COEF * (pre_act + CUBIC_COEF * pre_act * pre_act * pre_act)
    return 0.5 * pre_act * (1.0 + jnp.tanh(inner))


def gelu_slope(pre_act):
    inner = GELU_COEF * (pre_act + CUBIC_COEF * pre_act * pre_act * pre_act)
    tanh_val = jnp.tanh(inner)
    return 0.5 * (1.0 + tanh_val) + 0.5 * pre_act * (1.0 - tanh_val * tanh_val) * GELU_COEF * (1.0 + 3.0 * CUBIC_COEF * pre_act * pre_act)


def solution(mesh):
    act_spec = P(("dep", "row"), "col")
    wgt_spec = P("row", "col")
    grad_spec = P(("row", "dep"), "col")

    def local_block(x_loc, w_up_loc, w_down_loc, g_loc):
        x_full = lax.all_gather(x_loc, "col", axis=1, tiled=True)
        w_up_cols = lax.all_gather(w_up_loc, "row", axis=0, tiled=True)
        pre_act = jnp.dot(x_full, w_up_cols, preferred_element_type=jnp.float32)
        hidden_act = gelu_fwd(pre_act).astype(jnp.bfloat16)
        act_full = lax.all_gather(hidden_act, "col", axis=1, tiled=True)
        w_down_cols = lax.all_gather(w_down_loc, "row", axis=0, tiled=True)
        y_loc = jnp.dot(act_full, w_down_cols, preferred_element_type=jnp.float32).astype(jnp.bfloat16)
        d_act_part = jnp.einsum("th,fh->tf", g_loc, w_down_cols, preferred_element_type=jnp.float32)
        d_act = lax.psum_scatter(d_act_part, "col", scatter_dimension=1, tiled=True)
        d_pre = (d_act * gelu_slope(pre_act)).astype(jnp.bfloat16)
        dx_part = jnp.einsum("tf,hf->th", d_pre, w_up_cols, preferred_element_type=jnp.float32)
        dx_loc = lax.psum_scatter(dx_part, "col", scatter_dimension=1, tiled=True).astype(jnp.bfloat16)
        x_layer = lax.all_to_all(x_full, "row", 1, 0, tiled=True)
        d_pre_layer = lax.all_gather(d_pre, "row", axis=0, tiled=True)
        dw_up_part = jnp.einsum("th,tf->hf", x_layer, d_pre_layer, preferred_element_type=jnp.float32)
        dw_up_loc = lax.psum_scatter(dw_up_part, "dep", scatter_dimension=0, tiled=True)
        act_layer = lax.all_to_all(act_full, "row", 1, 0, tiled=True)
        g_layer = lax.all_gather(g_loc, "row", axis=0, tiled=True)
        dw_down_part = jnp.einsum("tf,th->fh", act_layer, g_layer, preferred_element_type=jnp.float32)
        dw_down_loc = lax.psum_scatter(dw_down_part, "dep", scatter_dimension=0, tiled=True)
        return y_loc, dx_loc, dw_up_loc, dw_down_loc

    return jax.shard_map(local_block, mesh=mesh, in_specs=(act_spec, wgt_spec, wgt_spec, act_spec), out_specs=(act_spec, act_spec, grad_spec, grad_spec), check_vma=False)
```

profile of v0, /device:TPU:0, one launch (start us, length us, event | category | flops | bytes accessed | tf_op | source)
XLA Modules:
  0.0 1684.7 jit_solution(3197936866585881505)
XLA Ops:
  7.2 0.7 all-gather.13.cloned.1.call-update
  7.9 0.7 all-gather.9.cloned.1.call-update
  8.6 0.0 all-gather.7.cloned.1.call-start
  8.7 6.3 copy.11
  15.0 0.0 reduce-scatter.5.cloned.1.call-start
  15.1 8.5 all-gather.13.cloned.1.call-done
  23.6 30.0 %fusion.7 = f32[4096,4096]{1,0:T(8,128)} fusion(bf16[4096,512]{1,0:T(8,128)(2,1)} %param.7, bf16[4096,512]{1,0:T(8,128)(2,1)} %all-gather.13.cloned.1.call-done), kind=kOutput, calls=%fused_computation.13 | convolution fusion | flops 17179869184 | bytes 75497472 | tf_op jit(solution)/shard_map/th,fh->tf/dot_general | solution.py:34
  53.6 0.2 all-gather.15.cloned.1.call-start
  53.9 89.2 %all-gather.7.cloned.1.call-done = bf16[4096,1024]{0,1:T(8,128)(2,1)} async-done(((bf16[4096,512]{0,1:T(8,128)(2,1)}), bf16[4096,1024]{0,1:T(8,128)(2,1)}) %all-gather.7.cloned.1.call-update) | async-done | bytes 8388624 | tf_op jit(solution)/shard_map/all_gather | solution.py:27
  143.1 727.8 %reduce-scatter.5.cloned.1.call-done = f32[4096,2048]{1,0:T(8,128)} async-done(((f32[4096,4096]{1,0:T(8,128)}), f32[4096,2048]{1,0:T(8,128)}) %reduce-scatter.5.cloned.1.call-update) | async-done | bytes 33554448 | tf_op jit(solution)/shard_map/reduce_scatter | solution.py:35
  870.8 47.3 %fusion.6 = (bf16[4096,2048]{1,0:T(8,128)(2,1)}, bf16[4096,2048]{1,0:T(8,128)(2,1)}) fusion(f32[4096,2048]{1,0:T(8,128)} %reduce-scatter.5.cloned.1.call-done, bf16[4096,1024]{0,1:T(8,128)(2,1)} %all-gather.7.cloned.1.call-done, bf16[1024,2048]{1,0:T(8,128)(2,1)} %all-gather.9.cloned.1.call-done), kind=kOutput, calls=%fused_computation.8 | convolution fusion | flops 17356029952 | bytes 79691776 | tf_op jit(solution)/shard_map/dot_general | solution.py:29
  918.1 0.0 all-gather.11.cloned.1.call-start
  918.2 0.5 all-gather.11.cloned.1.call-update
  918.8 0.7 all-gather.17.cloned.1.call-update
  919.5 0.3 reduce-scatter.7.cloned.1.call-start
  919.7 23.7 %fusion.8 = f32[4096,1024]{1,0:T(8,128)} fusion(bf16[4096,2048]{1,0:T(8,128)(2,1)} %get-tuple-element.16, bf16[1024,2048]{1,0:T(8,128)(2,1)} %all-gather.9.cloned.1.call-done), kind=kOutput, calls=%fused_computation.14 | convolution fusion | flops 17179869184 | bytes 37748736 | tf_op jit(solution)/shard_map/tf,hf->th/dot_general | solution.py:37
  943.4 0.0 reduce-scatter.9.cloned.1.call-start
  943.5 24.1 %all_to_all.38 = bf16[4096,2,512]{0,2,1:T(8,128)(2,1)} all-to-all(bf16[4096,2,512]{0,2,1:T(8,128)(2,1)} %bitcast.27), channel_id=1, replica_groups=mesh['dep'=2,'col'=2,'row'=2] {'row'}, dimensions={1} | all-to-all | bytes 16777216 | tf_op jit(solution)/shard_map/all_to_all | solution.py:39
  967.6 12.0 copy.12
  979.6 24.9 %convolution_bitcast_fusion = f32[512,2048]{0,1:T(8,128)} fusion(bf16[8192,2048]{1,0:T(8,128)(2,1)} %all-gather.15.cloned.1.call-done, bf16[8192,512]{1,0:T(8,128)(2,1)} %bitcast.28), kind=kOutput, calls=%fused_computation.12 | convolution fusion | flops 17179869184 | bytes 46137344 | tf_op jit(solution)/shard_map/th,tf->hf/dot_general | solution.py:41
  1004.5 356.0 %all-gather.11.cloned.1.call-done = bf16[4096,4096]{1,0:T(8,128)(2,1)} async-done(((bf16[4096,2048]{1,0:T(8,128)(2,1)}), bf16[4096,4096]{1,0:T(8,128)(2,1)}) %all-gather.11.cloned.1.call-update) | async-done | bytes 33554448 | tf_op jit(solution)/shard_map/all_gather | solution.py:31
  1360.5 23.0 %copy.17 = bf16[512,2,8,2048]{3,2,0,1:T(8,128)(2,1)} copy(bf16[512,2,8,2048]{3,2,1,0:T(8,128)(2,1)} %bitcast.25) | data formatting | bytes 67108864 | tf_op jit(solution)/shard_map/all_to_all | solution.py:43
  1383.5 13.1 all-to-all-start.1
  1396.6 0.3 reduce-scatter.11.cloned.1.call-start
  1396.9 24.7 %all-to-all-done.1 = bf16[4096,2,2048]{2,0,1:T(8,128)(2,1)} async-done(((bf16[4096,2,2048]{2,0,1:T(8,128)(2,1)}), bf16[4096,2,2048]{2,0,1:T(8,128)(2,1)}, u32[]{:S(2)}, u32[]{:S(2)}) %all-to-all-start.1) | async-done | bytes 33554464 | tf_op jit(solution)/shard_map/all_to_all | solution.py:43
  1421.7 24.9 %fusion.9 = f32[2048,512]{1,0:T(8,128)} fusion(bf16[8192,2048]{1,0:T(8,128)(2,1)} %bitcast.5, bf16[8192,512]{1,0:T(8,128)(2,1)} %all-gather.17.cloned.1.call-done), kind=kOutput, calls=%fused_computation.15 | convolution fusion | flops 17179869184 | bytes 46137344 | tf_op jit(solution)/shard_map/tf,th->fh/dot_general | solution.py:45
  1446.6 123.3 %reduce-scatter.7.cloned.1.call-done = f32[4096,512]{1,0:T(8,128)} async-done(((f32[4096,1024]{1,0:T(8,128)}), f32[4096,512]{1,0:T(8,128)}) %reduce-scatter.7.cloned.1.call-update) | async-done | bytes 8388624 | tf_op jit(solution)/shard_map/reduce_scatter | solution.py:38
  1569.8 5.9 convert_element_type.15
  1575.8 24.5 %convolution_convert_fusion = bf16[4096,512]{1,0:T(8,128)(2,1)} fusion(bf16[4096,4096]{1,0:T(8,128)(2,1)} %all-gather.11.cloned.1.call-done, bf16[4096,512]{1,0:T(8,128)(2,1)} %all-gather.13.cloned.1.call-done), kind=kOutput, calls=%fused_computation.11 | convolution fusion | flops 17181966336 | bytes 41943040 | tf_op jit(solution)/shard_map/dot_general | solution.py:33
  1600.2 23.4 %reduce-scatter.9.cloned.1.call-done = f32[256,2048]{0,1:T(8,128)} async-done(((f32[512,2048]{0,1:T(8,128)}), f32[256,2048]{0,1:T(8,128)}) %reduce-scatter.9.cloned.1.call-update) | async-done | bytes 2097168 | tf_op jit(solution)/shard_map/reduce_scatter | solution.py:42
  1623.7 2.9 copy.14
  1626.5 51.3 %reduce-scatter.11.cloned.1.call-done = f32[1024,512]{1,0:T(8,128)} async-done(((f32[2048,512]{1,0:T(8,128)}), f32[1024,512]{1,0:T(8,128)}) %reduce-scatter.11.cloned.1.call-update) | async-done | bytes 2097168 | tf_op jit(solution)/shard_map/reduce_scatter | solution.py:46
  (12 shorter events, 0.3 us)
Async XLA Ops:
  7.2 16.4 all-gather.13.cloned.1.call-start
  7.9 45.9 %all-gather.9.cloned.1.call-start = ((), (), s32[]{:S(2)}) async-start(), calls=%async_computation.7 | async-start | bytes 6291456 | tf_op jit(solution)/shard_map/all_gather | solution.py:28
  8.6 134.4 %all-gather.7.cloned.1.call-start = ((), (), s32[]{:S(2)}) async-start(), calls=%async_computation.6 | async-start | bytes 12582912 | tf_op jit(solution)/shard_map/all_gather | solution.py:27
  15.0 855.8 %reduce-scatter.5.cloned.1.call-start = ((), (), s32[]{:S(2)}) async-start(), calls=%async_computation.10 | async-start | bytes 100663296 | tf_op jit(solution)/shard_map/reduce_scatter | solution.py:35
  53.6 926.0 %all-gather.15.cloned.1.call-start = ((), (), s32[]{:S(2)}) async-start(), calls=%async_computation.12 | async-start | bytes 50331648 | tf_op jit(solution)/shard_map/all_gather | solution.py:40
  918.1 442.4 %all-gather.11.cloned.1.call-start = ((), (), s32[]{:S(2)}) async-start(), calls=%async_computation.8 | async-start | bytes 50331648 | tf_op jit(solution)/shard_map/all_gather | solution.py:31
  918.7 478.2 %all-gather.17.cloned.1.call-start = ((), (), s32[]{:S(2)}) async-start(), calls=%async_computation.14 | async-start | bytes 12582912 | tf_op jit(solution)/shard_map/all_gather | solution.py:44
  919.5 650.4 %reduce-scatter.7.cloned.1.call-start = ((), (), s32[]{:S(2)}) async-start(), calls=%async_computation.11 | async-start | bytes 25165824 | tf_op jit(solution)/shard_map/reduce_scatter | solution.py:38
  943.4 680.2 %reduce-scatter.9.cloned.1.call-start = ((), (), s32[]{:S(2)}) async-start(), calls=%async_computation.13 | async-start | bytes 6291456 | tf_op jit(solution)/shard_map/reduce_scatter | solution.py:42
  1383.5 38.2 %all-to-all-start.1 = ((bf16[4096,2,2048]{2,0,1:T(8,128)(2,1)}), bf16[4096,2,2048]{2,0,1:T(8,128)(2,1)}, u32[]{:S(2)}, u32[]{:S(2)}) async-start(bf16[4096,2,2048]{2,0,1:T(8,128)(2,1)} %bitcast.24), calls=%async_computation.4 | async-start | bytes 67108864 | tf_op jit(solution)/shard_map/all_to_all | solution.py:43
  1396.6 281.3 %reduce-scatter.11.cloned.1.call-start = ((), (), s32[]{:S(2)}) async-start(), calls=%async_computation.15 | async-start | bytes 6291456 | tf_op jit(solution)/shard_map/reduce_scatter | solution.py:46
Sparse Core Ops, SparseCore 0:
  9.5 14.0 all-gather.12
  25.1 12.3 all-gather.8
  39.6 103.4 all-gather.6
  145.2 725.6 reduce-scatter.4
  918.3 54.1 all-gather.14
  973.8 386.6 all-gather.10
  1362.0 18.0 all-gather.16
  1382.3 187.4 reduce-scatter.6
  1572.1 51.5 reduce-scatter.8
  1626.3 51.4 reduce-scatter.10
where the time goes:
time: 1690 us; the launch traced here: 1680 us
  waiting for transfers between devices  1410 us (83%)
  matrix products  175 us (10%)
  local copies, waits for them, and re-layouts  44.1 us (3%)
  blocking collectives  24.1 us (1%)
    reduce_scatter x1, waiting for transfers between devices, local_block(): d_act = lax.psum_scatter(d_act_part, 'col', scatter_dimension=1, tiled=True)  728 us
    all_gather x1, waiting for transfers between devices, local_block(): act_full = lax.all_gather(hidden_act, 'col', axis=1, tiled=True)  356 us
    reduce_scatter x1, waiting for transfers between devices, local_block(): lax.psum_scatter(dx_part, 'col', scatter_dimension=1, tiled=True)  123 us
    all_gather x1, waiting for transfers between devices, local_block(): x_full = lax.all_gather(x_loc, 'col', axis=1, tiled=True)  89.2 us
    reduce_scatter x1, waiting for transfers between devices, local_block(): lax.psum_scatter(dw_down_part, 'dep', scatter_dimension=0, tiled=True)  51.3 us
    dot_general x1, matrix products, local_block(): pre_act = jnp.dot(x_full, w_up_cols, preferred_element_type=jnp.float32)  47.3 us
  transfers between devices with their start and end apart: 11, of which 8 were waited for; matrix products, arithmetic and copies ran while one was open for 11% of the time, Pallas kernels for 0%

commit v1 on v0

v1 whole, which is shorter than its diff:
```python
import functools

import jax
import jax.numpy as jnp
from jax import lax
from jax.experimental import pallas as pl
from jax.experimental.pallas import tpu as pltpu
from jax.sharding import PartitionSpec as P

GELU_COEF = 0.7978845608028654
CUBIC_COEF = 0.044715
MESH = pl.DeviceIdType.MESH
F32, BF16 = jnp.float32, jnp.bfloat16
CHUNKS = 8
BLOCKS = 8
RING = 4
AHEAD = 4


def gelu_and_slope(u):
    u2 = u * u
    p = GELU_COEF * CUBIC_COEF * u2 + GELU_COEF
    s = 0.5 * jnp.tanh(u * p) + 0.5
    a = u * s
    return a, s + (a * (1.0 - s)) * (6.0 * GELU_COEF * CUBIC_COEF * u2 + 2.0 * GELU_COEF)


def dot(a, b, ca=1, cb=0):
    return lax.dot_general(a, b, (((ca,), (cb,)), ((), ())), preferred_element_type=F32)


def kernel(x_hbm, w1_hbm, w2_hbm, g_hbm, y_hbm, dx_hbm, dw1_own, dw1_got, dw2_own, dw2_got, slope_hbm,
           w1, w2, xf, gf, dw1, dw2t, ring, rbuf, acc, out_buf,
           load_sem, w_send, w_recv, x_send, x_recv, ring_sem, out_sem, row_send, row_recv, dep_send, dep_recv, own_sem, free_sem):
    d, c, r = lax.axis_index("dep"), lax.axis_index("col"), lax.axis_index("row")
    o = 1 - c
    across, layer, sibling = (d, o, r), (1 - d, c, r), (d, c, 1 - r)
    tokens, half = x_hbm.shape
    t = tokens // CHUNKS
    ffn = w1.shape[1]
    f = ffn // BLOCKS
    hf = BLOCKS // 2

    barrier = pltpu.get_barrier_semaphore()
    for peer in (across, layer, sibling):
        pl.semaphore_signal(barrier, inc=1, device_id=peer, device_id_type=MESH)
    pl.semaphore_wait(barrier, 3)

    def remote(src, dst, send, recv, dev):
        return pltpu.make_async_remote_copy(src_ref=src, dst_ref=dst, send_sem=send, recv_sem=recv, device_id=dev, device_id_type=MESH)

    def al(v, m):
        return pl.multiple_of(v, m)

    wts = ((w1_hbm, w1), (w2_hbm, w2))

    def w_copy(k, what):
        hbm, ref = wts[k]
        rows, cols = hbm.shape
        hr = rows // 2
        mine = lambda dep, col: ref.at[pl.ds(al(r * rows + dep * hr, hr), hr), pl.ds(al(col * cols, cols), cols)]
        if what == 0:
            return remote(hbm.at[pl.ds(al(d * hr, hr), hr), :], mine(d, c), w_send.at[k, 0], w_recv.at[k, 0], across)
        if what == 1:
            return remote(hbm, ref.at[pl.ds(al(r * rows, rows), rows), pl.ds(al(c * cols, cols), cols)], w_send.at[k, 1], w_recv.at[k, 1], sibling)
        if what == 2:
            return remote(mine(d, o), mine(d, o), w_send.at[k, 2], w_recv.at[k, 2], layer)
        if what == 3:
            return remote(mine(d, o), mine(d, o), w_send.at[k, 3], w_recv.at[k, 3], sibling)
        if what == 4:
            return remote(mine(1 - d, o), mine(1 - d, o), w_send.at[k, 4], w_recv.at[k, 4], sibling)
        return pltpu.make_async_copy(hbm, ref.at[pl.ds(al(r * rows, rows), rows), pl.ds(al(c * cols, cols), cols)], load_sem.at[k])

    acts = ((x_hbm, xf), (g_hbm, gf))

    def act_copy(k, i):
        hbm, ref = acts[k]
        rows = pl.ds(al(i * t, t), t)
        return remote(hbm.at[rows, :], ref.at[rows, pl.ds(al(c * half, half), half)], x_send.at[k, i], x_recv.at[k, i], across)

    def act_load(k):
        hbm, ref = acts[k]
        return pltpu.make_async_copy(hbm, ref.at[:, pl.ds(al(c * half, half), half)], load_sem.at[2 + k])

    for k in range(2):
        w_copy(k, 0).start()
        w_copy(k, 1).start()
        w_copy(k, 5).start()
    for k in range(2):
        act_load(k).start()
    for i in range(AHEAD):
        act_copy(0, i).start()

    dw1[...] = jnp.zeros_like(dw1)
    dw2t[...] = jnp.zeros_like(dw2t)
    for k in range(2):
        w_copy(k, 0).wait_recv()
        w_copy(k, 2).start()
        w_copy(k, 3).start()
    for k in range(2):
        w_copy(k, 5).wait()
        w_copy(k, 1).wait_recv()
        act_load(k).wait()
    w_copy(0, 2).wait_recv()
    w_copy(0, 4).start()
    w_copy(0, 3).wait_recv()
    w_copy(0, 4).wait_recv()

    def block_of(jj):
        return lax.rem(c * hf + jj, BLOCKS)

    def slope_copy(i, jj, slot, out):
        far = slope_hbm.at[i, jj]
        near = ring.at[slot]
        return pltpu.make_async_copy(near, far, ring_sem.at[slot]) if out else pltpu.make_async_copy(far, near, ring_sem.at[slot])

    def put(ref, i):
        return pltpu.make_async_copy(out_buf, ref.at[pl.ds(al(i * t, t), t), :], out_sem.at[0])

    own_cols = pl.ds(al(c * half, half), half)

    @pl.loop(0, CHUNKS)
    def _(i):
        rows = pl.ds(al(i * t, t), t)
        act_copy(0, i).wait_recv()

        @pl.when(i < CHUNKS - AHEAD)
        def _():
            act_copy(0, i + AHEAD).start()

        @pl.when(i >= CHUNKS - AHEAD)
        def _():
            act_copy(1, i + AHEAD - CHUNKS).start()

        @pl.loop(0, BLOCKS)
        def _(jj):
            n = i * BLOCKS + jj
            slot = lax.rem(n, RING)
            cols = pl.ds(al(block_of(jj) * f, f), f)
            u = dot(xf[rows, :], w1[:, cols])
            a, slope = gelu_and_slope(u)

            @pl.when(n >= RING)
            def _():
                slope_copy(i, jj, slot, True).wait()
            ring[slot] = slope
            slope_copy(i, jj, slot, True).start()
            a = a.astype(BF16)
            y = dot(a, w2[cols, own_cols])

            @pl.when(jj == 0)
            def _():
                acc[...] = y

            @pl.when(jj > 0)
            def _():
                acc[...] += y
            dw2t[:, cols] += dot(gf[rows, own_cols], a, 0, 0)

        @pl.when(i >= 1)
        def _():
            put(y_hbm, i).wait()
        out_buf[...] = acc[...].astype(BF16)
        put(y_hbm, i).start()

        @pl.when(i == 1)
        def _():
            w_copy(1, 2).wait_recv()
            w_copy(1, 4).start()
            w_copy(1, 3).wait_recv()

    for s in range(RING):
        slope_copy(0, 0, s, True).wait()
    for s in range(RING - 1):
        slope_copy(0, s, s, False).start()

    hcols = ffn // 2
    qcols = ffn // 4
    other_r = pl.ds(al((1 - r) * hcols, hcols), hcols)
    mine_r = pl.ds(al(r * hcols, hcols), hcols)

    def dw2_row():
        return remote(dw2t.at[:, other_r], rbuf, row_send.at[0], row_recv.at[0], sibling)

    def dw2_dep():
        return remote(dw2t.at[:, pl.ds(al(r * hcols + (1 - d) * qcols, qcols), qcols)], dw2_got, dep_send.at[0], dep_recv.at[0], layer)

    def dw2_out():
        return pltpu.make_async_copy(dw2t.at[:, pl.ds(al(r * hcols + d * qcols, qcols), qcols)], dw2_own, own_sem.at[0])

    dw2_row().start()
    w_copy(1, 4).wait_recv()
    put(y_hbm, 0).wait()
    dw2_row().wait_recv()
    dw2t[:, mine_r] += rbuf[...]
    pl.semaphore_signal(free_sem, inc=1, device_id=sibling, device_id_type=MESH)
    dw2_dep().start()
    dw2_out().start()

    @pl.loop(0, CHUNKS)
    def _(i):
        rows = pl.ds(al(i * t, t), t)
        act_copy(1, i).wait_recv()

        @pl.when(i < CHUNKS - AHEAD)
        def _():
            act_copy(1, i + AHEAD).start()

        def step(jj, with_dw1):
            n = i * BLOCKS + jj
            slot = lax.rem(n, RING)
            j = block_of(jj)
            cols = pl.ds(al(j * f, f), f)
            slope_copy(i, jj, slot, False).wait()

            @pl.when(n + RING - 1 < CHUNKS * BLOCKS)
            def _():
                m = n + RING - 1
                slope_copy(m // BLOCKS, lax.rem(m, BLOCKS), lax.rem(m, RING), False).start()
            da = dot(gf[rows, :], w2[cols, :], 1, 1)
            du = (da * ring[slot]).astype(BF16)
            dx = dot(du, w1[own_cols, cols], 1, 1)

            @pl.when(jj == 0)
            def _():
                acc[...] = dx

            @pl.when(jj > 0)
            def _():
                acc[...] += dx
            if with_dw1:
                dw1[:, pl.ds(al(jj * f, f), f)] += dot(xf[rows, :], du, 0, 0)

        @pl.loop(0, hf)
        def _(jj):
            step(jj, True)

        @pl.loop(hf, BLOCKS)
        def _(jj):
            step(jj, False)

        @pl.when(i >= 1)
        def _():
            put(dx_hbm, i).wait()
        out_buf[...] = acc[...].astype(BF16)
        put(dx_hbm, i).start()

    def dw1_row():
        return remote(dw1.at[pl.ds(al((1 - r) * half, half), half), :], rbuf, row_send.at[1], row_recv.at[1], sibling)

    q = half // 2

    def dw1_dep():
        return remote(dw1.at[pl.ds(al(r * half + (1 - d) * q, q), q), :], dw1_got, dep_send.at[1], dep_recv.at[1], layer)

    def dw1_out():
        return pltpu.make_async_copy(dw1.at[pl.ds(al(r * half + d * q, q), q), :], dw1_own, own_sem.at[1])

    pl.semaphore_wait(free_sem, 1)
    dw1_row().start()
    dw1_row().wait_recv()
    dw1[pl.ds(al(r * half, half), half), :] += rbuf[...]
    dw1_dep().start()
    dw1_out().start()

    for k in range(2):
        for what in range(5):
            w_copy(k, what).wait_send()
        for i in range(CHUNKS):
            act_copy(k, i).wait_send()
    put(dx_hbm, 0).wait()
    dw2_row().wait_send()
    dw2_dep().wait()
    dw2_out().wait()
    dw1_row().wait_send()
    dw1_dep().wait()
    dw1_out().wait()


def solution(mesh):
    act_spec = P(("dep", "row"), "col")
    wgt_spec = P("row", "col")
    grad_spec = P(("row", "dep"), "col")

    def local_block(x, w1, w2, g):
        tokens, half = x.shape
        hidden, hcols = w1.shape[0] * 2, w1.shape[1]
        ffn = hcols * 2
        t, f = tokens // CHUNKS, ffn // BLOCKS
        sds = jax.ShapeDtypeStruct
        dma = pltpu.SemaphoreType.DMA
        outs = pl.pallas_call(
            kernel,
            out_shape=[
                sds((tokens, half), BF16), sds((tokens, half), BF16),
                sds((half // 2, hcols), F32), sds((half // 2, hcols), F32),
                sds((half, ffn // 4), F32), sds((half, ffn // 4), F32),
                sds((CHUNKS, BLOCKS, t, f), F32),
            ],
            in_specs=[pl.BlockSpec(memory_space=pl.ANY)] * 4,
            out_specs=[pl.BlockSpec(memory_space=pl.ANY)] * 7,
            scratch_shapes=[
                pltpu.VMEM((hidden, ffn), BF16), pltpu.VMEM((ffn, hidden), BF16),
                pltpu.VMEM((tokens, hidden), BF16), pltpu.VMEM((tokens, hidden), BF16),
                pltpu.VMEM((hidden, hcols), F32), pltpu.VMEM((half, ffn), F32),
                pltpu.VMEM((RING, t, f), F32), pltpu.VMEM((half, hcols), F32),
                pltpu.VMEM((t, half), F32), pltpu.VMEM((t, half), BF16),
                dma((4,)), dma((2, 5)), dma((2, 5)), dma((2, CHUNKS)), dma((2, CHUNKS)),
                dma((RING,)), dma((2,)), dma((2,)), dma((2,)), dma((2,)), dma((2,)), dma((2,)),
                pltpu.SemaphoreType.REGULAR,
            ],
            compiler_params=pltpu.CompilerParams(collective_id=0, has_side_effects=True, vmem_limit_bytes=67043328),
            name="mlp_block",
        )(x, w1, w2, g)
        y, dx, dw1_own, dw1_got, dw2_own, dw2_got, _ = outs
        return y, dx, dw1_own + dw1_got, (dw2_own + dw2_got).T

    return jax.shard_map(local_block, mesh=mesh, in_specs=(act_spec, wgt_spec, wgt_spec, act_spec), out_specs=(act_spec, act_spec, grad_spec, grad_spec), check_vma=False)
```

time: 1690 us -> 367 us (0.22)
  waiting for transfers between devices: 1410 us -> 0 us
  Pallas kernels: 0 us -> 354 us
  matrix products: 175 us -> 0 us
  local copies, waits for them, and re-layouts: 44.1 us -> 8.48 us
  blocking collectives: 24.1 us -> 0 us
    reduce_scatter x4 -> x0, waiting for transfers between devices: 926 us -> none  [the longest x1 728 us: local_block(): d_act = lax.psum_scatter(d_act_part, 'col', scatter_dimension=1, tiled=True)]
    all_gather x6 -> x0, waiting for transfers between devices: 454 us -> none  [the longest x1 356 us: local_block(): act_full = lax.all_gather(hidden_act, 'col', axis=1, tiled=True)]
    pallas_call x0 -> x1, Pallas kernels: none -> 354 us  [local_block(): pl.pallas_call(kernel, out_shape=[sds((tokens, half), BF16), sds((tokens,...]
    dot_general x6 -> x0, matrix products: 175 us -> none  [the longest x1 47.3 us: local_block(): pre_act = jnp.dot(x_full, w_up_cols, preferred_element_type=jnp.float32)]
    all_to_all x2 -> x0, local copies, waits for them, and re-layouts: 34.9 us -> none  [the longest x1 23 us: local_block(): act_layer = lax.all_to_all(act_full, 'row', 1, 0, tiled=True)]
    all_to_all x1 -> x0, waiting for transfers between devices: 24.7 us -> none  [local_block(): act_layer = lax.all_to_all(act_full, 'row', 1, 0, tiled=True)]
    all_to_all x1 -> x0, blocking collectives: 24.1 us -> none  [local_block(): x_layer = lax.all_to_all(x_full, 'row', 1, 0, tiled=True)]
  transfers between devices with their start and end apart: 11 -> 0, of which waited for: 8 -> 0; matrix products, arithmetic and copies ran while one was open for 11% -> 0% of each run, Pallas kernels for 0% -> 0%
where the time goes in v1:
time: 367 us
  Pallas kernels  354 us (96%)
  local copies, waits for them, and re-layouts  8.48 us (2%)
  other arithmetic  4.42 us (1%)
    pallas_call x1, Pallas kernels, local_block(): pl.pallas_call(kernel, out_shape=[sds((tokens, half), BF16), sds((tokens,...  354 us
    unnamed x9, local copies, waits for them, and re-layouts  8.48 us

profile of v1, /device:TPU:0, one launch (start us, length us, event | category | flops | bytes accessed | tf_op | source)
XLA Modules:
  0.0 367.3 jit_solution(14360139375588090066)
XLA Ops:
  0.6 353.7 %mlp_block.1 = (bf16[4096,512]{1,0:T(8,128)(2,1)}, bf16[4096,512]{1,0:T(8,128)(2,1)}, f32[256,2048]{1,0:T(8,128)}, f32[256,2048]{1,0:T(8,128)}, f32[512,1024]{1,...) custom-call(bf16[4096,512]{1,0:T(8,128)(2,1)} %x_hbm.1, bf16[512,2048]{1,0:T(8,128)(2,1)} %w1_hbm.1, ...), custom_call_target="tpu_custom_call" | custom-call | tf_op jit(solution)/shard_map/mlp_block/pallas_call | solution.py:292
  354.3 0.0 copy-start.1
  354.3 0.0 copy-start.2
  354.3 4.0 %add.6 = f32[256,2048]{1,0:T(8,128)} add(f32[256,2048]{1,0:T(8,128)} %get-tuple-element.12, f32[256,2048]{1,0:T(8,128)} %get-tuple-element.13) | non-fusion elementwise | flops 524288 | bytes 6291456 | tf_op jit(solution)/shard_map/add | solution.py:316
  358.4 0.0 copy-done.1
  358.4 0.0 copy-done.2
  358.4 0.4 add_bitcast_fusion
  358.8 1.8 copy.8
  360.6 0.0 copy-start
  360.6 4.6 %copy.11 = bf16[4096,512]{1,0:T(8,128)(2,1)} copy(bf16[4096,512]{1,0:T(8,128)(2,1)} %get-tuple-element.24) | data formatting | bytes 8388608
  365.2 0.0 copy-done
  365.2 2.0 copy.12
Async XLA Ops:
  354.3 4.1 %copy-start.1 = (f32[512,1024]{1,0:T(8,128)S(1)}, f32[512,1024]{1,0:T(8,128)}, u32[]{:S(2)}) copy-start(f32[512,1024]{1,0:T(8,128)} %get-tuple-element.14) | copy-start | bytes 6291460
  354.3 4.0 %copy-start.2 = (f32[512,1024]{1,0:T(8,128)S(1)}, f32[512,1024]{1,0:T(8,128)}, u32[]{:S(2)}) copy-start(f32[512,1024]{1,0:T(8,128)} %get-tuple-element.15) | copy-start | bytes 6291460
  360.6 4.6 %copy-start = (bf16[4096,512]{1,0:T(8,128)(2,1)S(1)}, bf16[4096,512]{1,0:T(8,128)(2,1)}, u32[]{:S(2)}) copy-start(bf16[4096,512]{1,0:T(8,128)(2,1)} %get-tuple-element.25) | copy-start | bytes 12582916

commit v2 on v1

v2 whole, which is shorter than its diff:
```python
import functools

import jax
import jax.numpy as jnp
from jax import lax
from jax.experimental import pallas as pl
from jax.experimental.pallas import tpu as pltpu
from jax.sharding import PartitionSpec as P

GELU_COEF = 0.7978845608028654
CUBIC_COEF = 0.044715
MESH = pl.DeviceIdType.MESH
F32, BF16 = jnp.float32, jnp.bfloat16
CHUNKS = 8
BLOCKS = 8
RING = 4
AHEAD = 4


def gelu_and_slope(u):
    u2 = u * u
    p = GELU_COEF * CUBIC_COEF * u2 + GELU_COEF
    s = 0.5 * jnp.tanh(u * p) + 0.5
    a = u * s
    return a, s + (a * (1.0 - s)) * (6.0 * GELU_COEF * CUBIC_COEF * u2 + 2.0 * GELU_COEF)


def dot(a, b, ca=1, cb=0):
    return lax.dot_general(a, b, (((ca,), (cb,)), ((), ())), preferred_element_type=F32)


def kernel(x_hbm, w1_hbm, w2_hbm, g_hbm, y_hbm, dx_hbm, dw1_own, dw1_got, dw2_own, dw2_got, slope_hbm, part_hbm,
           w1, w2, xf, gf, dw1, dw2t, ring, acc, out_buf,
           load_sem, w_send, w_recv, x_send, x_recv, ring_sem, acc_sem, out_sem, row_send, row_recv, dep_send, dep_recv, own_sem, free_sem):
    d, c, r = lax.axis_index("dep"), lax.axis_index("col"), lax.axis_index("row")
    o = 1 - c
    across, layer, sibling = (d, o, r), (1 - d, c, r), (d, c, 1 - r)
    tokens, half = x_hbm.shape
    t = tokens // CHUNKS
    ffn = w1.shape[1]
    f = ffn // BLOCKS
    hf = BLOCKS // 2
    hcols, qcols, q = ffn // 2, ffn // 4, half // 2

    barrier = pltpu.get_barrier_semaphore()
    for peer in (across, layer, sibling):
        pl.semaphore_signal(barrier, inc=1, device_id=peer, device_id_type=MESH)
    pl.semaphore_wait(barrier, 3)

    def remote(src, dst, send, recv, dev):
        return pltpu.make_async_remote_copy(src_ref=src, dst_ref=dst, send_sem=send, recv_sem=recv, device_id=dev, device_id_type=MESH)

    def al(v, m):
        return pl.multiple_of(v, m)

    wts = ((w1_hbm, w1), (w2_hbm, w2))

    def w_copy(k, what):
        hbm, ref = wts[k]
        rows, cols = hbm.shape
        hr = rows // 2

        def part(dep, col):
            return ref.at[pl.ds(al(r * rows + dep * hr, hr), hr), pl.ds(al(col * cols, cols), cols)]

        def whole(col):
            return ref.at[pl.ds(al(r * rows, rows), rows), pl.ds(al(col * cols, cols), cols)]

        if what == 5:
            return pltpu.make_async_copy(hbm, whole(c), load_sem.at[k])
        src, dst, dev = (
            (hbm.at[pl.ds(al(d * hr, hr), hr), :], part(d, c), across),
            (hbm, whole(c), sibling),
            (part(d, o), part(d, o), layer),
            (part(d, o), part(d, o), sibling),
            (part(1 - d, o), part(1 - d, o), sibling),
            None,
            (hbm, whole(c), across),
            (whole(o), whole(o), sibling),
        )[what]
        return remote(src, dst, w_send.at[k, what], w_recv.at[k, what], dev)

    acts = ((x_hbm, xf), (g_hbm, gf))

    def act_copy(k, i):
        hbm, ref = acts[k]
        rows = pl.ds(al(i * t, t), t)
        return remote(hbm.at[rows, :], ref.at[rows, pl.ds(al(c * half, half), half)], x_send.at[k, i], x_recv.at[k, i], across)

    def act_load(k):
        hbm, ref = acts[k]
        return pltpu.make_async_copy(hbm, ref.at[:, pl.ds(al(c * half, half), half)], load_sem.at[2 + k])

    w_copy(0, 0).start()
    for i in range(AHEAD):
        act_copy(0, i).start()
    for k in range(2):
        w_copy(k, 5).start()
        w_copy(k, 1).start()
    for k in range(2):
        act_load(k).start()
    dw2t[...] = jnp.zeros_like(dw2t)
    w_copy(0, 0).wait_recv()
    w_copy(0, 2).start()
    w_copy(0, 3).start()
    for k in range(2):
        w_copy(k, 5).wait()
        w_copy(k, 1).wait_recv()
        act_load(k).wait()

    def block_of(jj):
        return lax.rem(c * hf + jj, BLOCKS)

    def slope_out(i, jj, slot):
        return pltpu.make_async_copy(ring.at[slot], slope_hbm.at[i, jj], ring_sem.at[slot])

    def slope_in(m):
        n = lax.rem(m, CHUNKS * hf)
        jj = (m // (CHUNKS * hf)) * hf + lax.rem(n, hf)
        slot = lax.rem(m, RING)
        return pltpu.make_async_copy(slope_hbm.at[n // hf, jj], ring.at[slot], ring_sem.at[slot])

    def put(ref, i):
        return pltpu.make_async_copy(out_buf, ref.at[pl.ds(al(i * t, t), t), :], out_sem.at[0])

    own_cols = pl.ds(al(c * half, half), half)

    @pl.loop(0, CHUNKS)
    def _(i):
        rows = pl.ds(al(i * t, t), t)
        act_copy(0, i).wait_recv()

        @pl.when(i < CHUNKS - AHEAD)
        def _():
            act_copy(0, i + AHEAD).start()

        @pl.when((i == CHUNKS - AHEAD) & (r != c))
        def _():
            w_copy(1, 0).start()

        @pl.when(i >= CHUNKS - AHEAD)
        def _():
            act_copy(1, i + AHEAD - CHUNKS).start()

        acc[0] = jnp.zeros_like(acc[0])

        @pl.loop(0, BLOCKS)
        def _(jj):
            n = i * BLOCKS + jj
            slot = lax.rem(n, RING)
            cols = pl.ds(al(block_of(jj) * f, f), f)

            @pl.when(n >= RING)
            def _():
                slope_out(i, jj, slot).wait()

            @pl.when(n == hf)
            def _():
                w_copy(0, 2).wait_recv()
                w_copy(0, 4).start()
                w_copy(0, 3).wait_recv()
                w_copy(0, 4).wait_recv()

            u = dot(xf[rows, :], w1[:, cols])
            a, slope = gelu_and_slope(u)
            ring[slot] = slope
            a = a.astype(BF16)
            acc[0] += dot(a, w2[cols, own_cols])
            dw2t[:, cols] += dot(gf[rows, own_cols], a, 0, 0)
            slope_out(i, jj, slot).start()

        @pl.when(i >= 1)
        def _():
            put(y_hbm, i).wait()
        out_buf[...] = acc[0].astype(BF16)
        put(y_hbm, i).start()

    other_r = pl.ds(al((1 - r) * hcols, hcols), hcols)
    mine_r = pl.ds(al(r * hcols, hcols), hcols)
    landing = dw1.at[0:half, :]

    def dw2_row():
        return remote(dw2t.at[:, other_r], landing, row_send.at[0], row_recv.at[0], sibling)

    def dw2_dep():
        return remote(dw2t.at[:, pl.ds(al(r * hcols + (1 - d) * qcols, qcols), qcols)], dw2_got, dep_send.at[0], dep_recv.at[0], layer)

    def dw2_out():
        return pltpu.make_async_copy(dw2t.at[:, pl.ds(al(r * hcols + d * qcols, qcols), qcols)], dw2_own, own_sem.at[0])

    dw2_row().start()
    for s in range(RING):
        slope_out(0, 0, s).wait()
    for m in range(RING - 1):
        slope_in(m).start()
    put(y_hbm, 0).wait()

    @pl.when(r == c)
    def _():
        w_copy(1, 0).wait_recv()
        w_copy(1, 2).start()
        w_copy(1, 3).start()

    dw2_row().wait_recv()
    dw2t[:, mine_r] += landing[...]
    dw2_dep().start()
    dw2_out().start()
    dw1[...] = jnp.zeros_like(dw1)

    @pl.when(r == c)
    def _():
        w_copy(1, 2).wait_recv()
        w_copy(1, 4).start()

    @pl.when(r != c)
    def _():
        w_copy(1, 3).wait_recv()
        w_copy(1, 4).wait_recv()

    def backward(i, jj, m, slot):
        rows = pl.ds(al(i * t, t), t)
        cols = pl.ds(al(block_of(jj) * f, f), f)
        slope_in(m).wait()

        @pl.when(m + RING - 1 < CHUNKS * BLOCKS)
        def _():
            slope_in(m + RING - 1).start()
        da = dot(gf[rows, :], w2[cols, :], 1, 1)
        du = (da * ring[lax.rem(m, RING)]).astype(BF16)
        acc[slot] += dot(du, w1[own_cols, cols], 1, 1)
        return rows, du

    def part_copy(i, out):
        far, near, sem = part_hbm.at[i], acc.at[lax.rem(i, 2)], acc_sem.at[lax.rem(i, 2)]
        return pltpu.make_async_copy(near, far, sem) if out else pltpu.make_async_copy(far, near, sem)

    @pl.loop(0, CHUNKS)
    def _(i):
        slot = lax.rem(i, 2)

        @pl.when(i >= 2)
        def _():
            part_copy(i, True).wait()
        act_copy(1, i).wait_recv()

        @pl.when(i < CHUNKS - AHEAD)
        def _():
            act_copy(1, i + AHEAD).start()

        @pl.when((i == CHUNKS - AHEAD) & (r == c))
        def _():
            w_copy(1, 6).start()

        @pl.when(i == CHUNKS - 2)
        def _():
            dw2_row().wait_send()
            dw2_dep().wait_send()
            dw2_out().wait()
            pl.semaphore_signal(free_sem, inc=1, device_id=sibling, device_id_type=MESH)

        acc[slot] = jnp.zeros_like(acc[slot])

        @pl.loop(0, hf)
        def _(jj):
            rows, du = backward(i, jj, i * hf + jj, slot)
            dw1[:, pl.ds(al(jj * f, f), f)] += dot(xf[rows, :], du, 0, 0)

        part_copy(i, True).start()

    def dw1_row(b):
        cols = pl.ds(b * f, f)
        return remote(dw1.at[pl.ds(al((1 - r) * half, half), half), cols], dw2t.at[:, cols], row_send.at[1 + b], row_recv.at[1 + b], sibling)

    def dw1_dep(b):
        cols = pl.ds(b * f, f)
        return remote(dw1.at[pl.ds(al(r * half + (1 - d) * q, q), q), cols], dw1_got.at[:, cols], dep_send.at[1 + b], dep_recv.at[1 + b], layer)

    def dw1_out():
        return pltpu.make_async_copy(dw1.at[pl.ds(al(r * half + d * q, q), q), :], dw1_own, own_sem.at[1])

    pl.semaphore_wait(free_sem, 1)
    for b in range(hf):
        dw1_row(b).start()
    for b in range(hf):
        dw1_row(b).wait_recv()
        dw1[pl.ds(al(r * half, half), half), b * f:(b + 1) * f] += dw2t[:, b * f:(b + 1) * f]
        dw1_dep(b).start()
    dw1_out().start()

    @pl.when(r != c)
    def _():
        w_copy(1, 6).wait_recv()
        w_copy(1, 7).start()

    @pl.when(r == c)
    def _():
        w_copy(1, 7).wait_recv()

    for i in (0, 1):
        part_copy(i, True).wait()
    part_copy(0, False).start()

    @pl.loop(0, CHUNKS)
    def _(i):
        slot = lax.rem(i, 2)
        part_copy(i, False).wait()

        @pl.when(i < CHUNKS - 1)
        def _():
            part_copy(i + 1, False).start()

        @pl.loop(0, hf)
        def _(jj):
            backward(i, hf + jj, CHUNKS * hf + i * hf + jj, slot)

        @pl.when(i >= 1)
        def _():
            put(dx_hbm, i).wait()
        out_buf[...] = acc[slot].astype(BF16)
        put(dx_hbm, i).start()

    for what in (0, 1, 2, 3, 4):
        w_copy(0, what).wait_send()
    w_copy(1, 1).wait_send()

    @pl.when(r != c)
    def _():
        w_copy(1, 0).wait_send()
        w_copy(1, 7).wait_send()

    @pl.when(r == c)
    def _():
        for what in (2, 3, 4, 6):
            w_copy(1, what).wait_send()

    for k in range(2):
        for i in range(CHUNKS):
            act_copy(k, i).wait_send()
    put(dx_hbm, 0).wait()
    dw2_dep().wait_recv()
    for b in range(hf):
        dw1_row(b).wait_send()
        dw1_dep(b).wait()
    dw1_out().wait()


def solution(mesh):
    act_spec = P(("dep", "row"), "col")
    wgt_spec = P("row", "col")
    grad_spec = P(("row", "dep"), "col")

    def local_block(x, w1, w2, g):
        tokens, half = x.shape
        hidden, hcols = w1.shape[0] * 2, w1.shape[1]
        ffn = hcols * 2
        t, f = tokens // CHUNKS, ffn // BLOCKS
        sds = jax.ShapeDtypeStruct
        dma = pltpu.SemaphoreType.DMA
        outs = pl.pallas_call(
            kernel,
            out_shape=[
                sds((tokens, half), BF16), sds((tokens, half), BF16),
                sds((half // 2, hcols), F32), sds((half // 2, hcols), F32),
                sds((half, ffn // 4), F32), sds((half, ffn // 4), F32),
                sds((CHUNKS, BLOCKS, t, f), F32), sds((CHUNKS, t, half), F32),
            ],
            in_specs=[pl.BlockSpec(memory_space=pl.ANY)] * 4,
            out_specs=[pl.BlockSpec(memory_space=pl.ANY)] * 8,
            scratch_shapes=[
                pltpu.VMEM((hidden, ffn), BF16), pltpu.VMEM((ffn, hidden), BF16),
                pltpu.VMEM((tokens, hidden), BF16), pltpu.VMEM((tokens, hidden), BF16),
                pltpu.VMEM((hidden, hcols), F32), pltpu.VMEM((half, ffn), F32),
                pltpu.VMEM((RING, t, f), F32), pltpu.VMEM((2, t, half), F32), pltpu.VMEM((t, half), BF16),
                dma((4,)), dma((2, 8)), dma((2, 8)), dma((2, CHUNKS)), dma((2, CHUNKS)),
                dma((RING,)), dma((2,)), dma((1,)),
                dma((1 + BLOCKS // 2,)), dma((1 + BLOCKS // 2,)), dma((1 + BLOCKS // 2,)), dma((1 + BLOCKS // 2,)), dma((2,)),
                pltpu.SemaphoreType.REGULAR,
            ],
            compiler_params=pltpu.CompilerParams(collective_id=0, has_side_effects=True, vmem_limit_bytes=67043328),
            name="mlp_block",
        )(x, w1, w2, g)
        y, dx, dw1_own, dw1_got, dw2_own, dw2_got, _, _ = outs
        return y, dx, dw1_own + dw1_got, (dw2_own + dw2_got).T

    return jax.shard_map(local_block, mesh=mesh, in_specs=(act_spec, wgt_spec, wgt_spec, act_spec), out_specs=(act_spec, act_spec, grad_spec, grad_spec), check_vma=False)
```

time: 367 us -> 295 us (0.80)
  Pallas kernels: 354 us -> 281 us
    pallas_call x1, Pallas kernels: 354 us -> 281 us  [local_block(): pl.pallas_call(kernel, out_shape=[sds((tokens, half), BF16), sds((tokens,...]
where the time goes in v2:
time: 295 us
  Pallas kernels  281 us (95%)
  local copies, waits for them, and re-layouts  8.48 us (3%)
  other arithmetic  4.42 us (1%)
    pallas_call x1, Pallas kernels, local_block(): pl.pallas_call(kernel, out_shape=[sds((tokens, half), BF16), sds((tokens,...  281 us
    unnamed x9, local copies, waits for them, and re-layouts  8.48 us

profile of v2, /device:TPU:0, one launch (start us, length us, event | category | flops | bytes accessed | tf_op | source)
XLA Modules:
  0.0 295.0 jit_solution(6428593072164771325)
XLA Ops:
  0.6 281.4 %mlp_block.1 = (bf16[4096,512]{1,0:T(8,128)(2,1)}, bf16[4096,512]{1,0:T(8,128)(2,1)}, f32[256,2048]{1,0:T(8,128)}, f32[256,2048]{1,0:T(8,128)}, f32[512,1024]{1,...) custom-call(bf16[4096,512]{1,0:T(8,128)(2,1)} %x_hbm.1, ...), custom_call_target="tpu_custom_call" | custom-call | tf_op jit(solution)/shard_map/mlp_block/pallas_call | solution.py:359
  282.1 0.0 copy-start.1
  282.1 0.0 copy-start.2
  282.1 4.0 %add.6 = f32[256,2048]{1,0:T(8,128)} add(f32[256,2048]{1,0:T(8,128)} %get-tuple-element.12, f32[256,2048]{1,0:T(8,128)} %get-tuple-element.13) | non-fusion elementwise | flops 524288 | bytes 6291456 | tf_op jit(solution)/shard_map/add | solution.py:383
  286.1 0.0 copy-done.1
  286.1 0.0 copy-done.2
  286.1 0.4 add_bitcast_fusion
  286.5 1.8 copy.8
  288.4 0.0 copy-start
  288.4 4.6 %copy.11 = bf16[4096,512]{1,0:T(8,128)(2,1)} copy(bf16[4096,512]{1,0:T(8,128)(2,1)} %get-tuple-element.24) | data formatting | bytes 8388608
  293.0 0.0 copy-done
  293.0 2.0 copy.12
Async XLA Ops:
  282.1 4.1 %copy-start.1 = (f32[512,1024]{1,0:T(8,128)S(1)}, f32[512,1024]{1,0:T(8,128)}, u32[]{:S(2)}) copy-start(f32[512,1024]{1,0:T(8,128)} %get-tuple-element.14) | copy-start | bytes 6291460
  282.1 4.0 %copy-start.2 = (f32[512,1024]{1,0:T(8,128)S(1)}, f32[512,1024]{1,0:T(8,128)}, u32[]{:S(2)}) copy-start(f32[512,1024]{1,0:T(8,128)} %get-tuple-element.15) | copy-start | bytes 6291460
  288.4 4.6 %copy-start = (bf16[4096,512]{1,0:T(8,128)(2,1)S(1)}, bf16[4096,512]{1,0:T(8,128)(2,1)}, u32[]{:S(2)}) copy-start(bf16[4096,512]{1,0:T(8,128)(2,1)} %get-tuple-element.25) | copy-start | bytes 12582916

commit v3 on v2

v3 whole, which is shorter than its diff:
```python
import functools

import jax
import jax.numpy as jnp
from jax import lax
from jax.experimental import pallas as pl
from jax.experimental.pallas import tpu as pltpu
from jax.sharding import PartitionSpec as P

GELU_COEF = 0.7978845608028654
CUBIC_COEF = 0.044715
MESH = pl.DeviceIdType.MESH
F32, BF16 = jnp.float32, jnp.bfloat16
CHUNKS = 8
BLOCKS = 8
RING = 4
AHEAD = 4
SLOTS = 4
PIECES = 4


def gelu_and_slope(u):
    u2 = u * u
    p = GELU_COEF * CUBIC_COEF * u2 + GELU_COEF
    s = 0.5 * jnp.tanh(u * p) + 0.5
    a = u * s
    return a, s + (a * (1.0 - s)) * (6.0 * GELU_COEF * CUBIC_COEF * u2 + 2.0 * GELU_COEF)


def dot(a, b, ca=1, cb=0):
    return lax.dot_general(a, b, (((ca,), (cb,)), ((), ())), preferred_element_type=F32)


def kernel(x_hbm, w1_hbm, w2_hbm, g_hbm, y_hbm, dx_hbm, dw1_own, dw2_own, slope_hbm, part_hbm,
           w1, w2, xf, gf, dw1, dw2t, ring, acc, out_buf,
           load_sem, w_send, w_recv, x_send, x_recv, ring_sem, acc_sem, out_sem, row_send, row_recv, dep_send, dep_recv, own_sem, free_sem, room_sem):
    d, c, r = lax.axis_index("dep"), lax.axis_index("col"), lax.axis_index("row")
    o = 1 - c
    across, layer, sibling = (d, o, r), (1 - d, c, r), (d, c, 1 - r)
    tokens, half = x_hbm.shape
    t = tokens // CHUNKS
    ffn = w1.shape[1]
    f = ffn // BLOCKS
    hf = BLOCKS // 2
    hcols, qcols, q = ffn // 2, ffn // 4, half // 2

    barrier = pltpu.get_barrier_semaphore()
    for peer in (across, layer, sibling):
        pl.semaphore_signal(barrier, inc=1, device_id=peer, device_id_type=MESH)
    pl.semaphore_wait(barrier, 3)

    def remote(src, dst, send, recv, dev):
        return pltpu.make_async_remote_copy(src_ref=src, dst_ref=dst, send_sem=send, recv_sem=recv, device_id=dev, device_id_type=MESH)

    def al(v, m):
        return pl.multiple_of(v, m)

    wts = ((w1_hbm, w1), (w2_hbm, w2))

    def w_copy(k, what):
        hbm, ref = wts[k]
        rows, cols = hbm.shape

        def span(start, size, col):
            return ref.at[pl.ds(al(start, size), size), pl.ds(al(col * cols, cols), cols)]

        def part(dep, col):
            if k == 0:
                return span(r * rows + dep * (rows // 2), rows // 2, col)
            return span((1 - col) * rows + dep * (rows // 2) + r * (rows // 4), rows // 4, col)

        def late(col):
            return span(col * rows + (what // 8) * (rows // 2) + r * (rows // 4), rows // 4, col)

        block = span(r * rows, rows, c)
        if what == 5:
            return pltpu.make_async_copy(hbm, block, load_sem.at[k])
        if what >= 6:
            src, dst, dev = (late(c), late(c), across) if what % 2 == 0 else (late(o), late(o), sibling)
        else:
            src, dst, dev = (
                (hbm.at[pl.ds(al(d * (rows // 2), rows // 2), rows // 2), :] if k == 0 else part(d, c), part(d, c), across),
                (hbm, block, sibling),
                (part(d, o), part(d, o), layer),
                (part(d, o), part(d, o), sibling),
                (part(1 - d, o), part(1 - d, o), sibling),
            )[what]
        return remote(src, dst, w_send.at[k, what], w_recv.at[k, what], dev)

    acts = ((x_hbm, xf), (g_hbm, gf))

    def act_copy(k, i):
        hbm, ref = acts[k]
        rows = pl.ds(al(i * t, t), t)
        return remote(hbm.at[rows, :], ref.at[rows, pl.ds(al(c * half, half), half)], x_send.at[k, i], x_recv.at[k, i], across)

    def act_load(k):
        hbm, ref = acts[k]
        return pltpu.make_async_copy(hbm, ref.at[:, pl.ds(al(c * half, half), half)], load_sem.at[2 + k])

    w_copy(0, 0).start()
    for i in range(AHEAD):
        act_copy(0, i).start()
    for k in range(2):
        w_copy(k, 5).start()
        w_copy(k, 1).start()
    for k in range(2):
        act_load(k).start()
    dw2t[...] = jnp.zeros_like(dw2t)
    w_copy(0, 0).wait_recv()
    w_copy(0, 2).start()
    w_copy(0, 3).start()
    for k in range(2):
        w_copy(k, 5).wait()
        w_copy(k, 1).wait_recv()
        act_load(k).wait()

    def block_of(jj):
        return lax.rem(c * hf + jj, BLOCKS)

    def slope_out(i, jj, slot):
        return pltpu.make_async_copy(ring.at[slot], slope_hbm.at[i, jj], ring_sem.at[slot])

    def slope_in(m):
        first = CHUNKS * hf
        n = jnp.maximum(m - first, 0)
        i = jnp.where(m < first, m // hf, lax.rem(n, first // 2) // 2)
        jj = jnp.where(m < first, lax.rem(m, hf), hf + (n // (first // 2)) * 2 + lax.rem(n, 2))
        slot = lax.rem(m, RING)
        return pltpu.make_async_copy(slope_hbm.at[i, jj], ring.at[slot], ring_sem.at[slot])

    def put(ref, i):
        return pltpu.make_async_copy(out_buf, ref.at[pl.ds(al(i * t, t), t), :], out_sem.at[0])

    own_cols = pl.ds(al(c * half, half), half)

    @pl.loop(0, CHUNKS)
    def _(i):
        rows = pl.ds(al(i * t, t), t)
        act_copy(0, i).wait_recv()

        @pl.when(i < CHUNKS - AHEAD)
        def _():
            act_copy(0, i + AHEAD).start()

        @pl.when(i == CHUNKS - AHEAD)
        def _():
            w_copy(1, 0).start()

        @pl.when(i >= CHUNKS - AHEAD)
        def _():
            act_copy(1, i + AHEAD - CHUNKS).start()

        acc[0] = jnp.zeros_like(acc[0])

        @pl.loop(0, BLOCKS)
        def _(jj):
            n = i * BLOCKS + jj
            slot = lax.rem(n, RING)
            cols = pl.ds(al(block_of(jj) * f, f), f)

            @pl.when(n >= RING)
            def _():
                slope_out(i, jj, slot).wait()

            @pl.when(n == hf)
            def _():
                w_copy(0, 2).wait_recv()
                w_copy(0, 4).start()
                w_copy(0, 3).wait_recv()
                w_copy(0, 4).wait_recv()

            u = dot(xf[rows, :], w1[:, cols])
            a, slope = gelu_and_slope(u)
            ring[slot] = slope
            a = a.astype(BF16)
            acc[0] += dot(a, w2[cols, own_cols])
            dw2t[:, cols] += dot(gf[rows, own_cols], a, 0, 0)
            slope_out(i, jj, slot).start()

        @pl.when(i >= 1)
        def _():
            put(y_hbm, i).wait()
        out_buf[...] = acc[0].astype(BF16)
        put(y_hbm, i).start()

    other_r = pl.ds(al((1 - r) * hcols, hcols), hcols)
    mine_r = pl.ds(al(r * hcols, hcols), hcols)
    landing = dw1.at[0:half, :]

    def dw2_row():
        return remote(dw2t.at[:, other_r], landing, row_send.at[0], row_recv.at[0], sibling)

    dw2_landing = pl.ds(al((1 - r) * hcols, hcols), qcols)
    dw2_mine = pl.ds(al(r * hcols + d * qcols, qcols), qcols)

    def dw2_dep():
        return remote(dw2t.at[:, pl.ds(al(r * hcols + (1 - d) * qcols, qcols), qcols)], dw2t.at[:, dw2_landing], dep_send.at[0], dep_recv.at[0], layer)

    def dw2_out():
        return pltpu.make_async_copy(dw2t.at[:, dw2_mine], dw2_own, own_sem.at[0])

    dw2_row().start()
    for s in range(RING):
        slope_out(0, 0, s).wait()
    for m in range(RING - 1):
        slope_in(m).start()
    put(y_hbm, 0).wait()

    w_copy(1, 0).wait_recv()
    w_copy(1, 2).start()
    w_copy(1, 3).start()
    dw2_row().wait()
    pl.semaphore_signal(room_sem, inc=1, device_id=layer, device_id_type=MESH)
    dw2t[:, mine_r] += landing[...]
    pl.semaphore_wait(room_sem, 1)
    dw2_dep().start()
    dw1[...] = jnp.zeros_like(dw1)

    w_copy(1, 2).wait_recv()
    w_copy(1, 4).start()
    w_copy(1, 3).wait_recv()
    w_copy(1, 4).wait_recv()

    def backward(i, jj, m, slot):
        rows = pl.ds(al(i * t, t), t)
        cols = pl.ds(al(block_of(jj) * f, f), f)
        slope_in(m).wait()

        @pl.when(m + RING - 1 < CHUNKS * BLOCKS)
        def _():
            slope_in(m + RING - 1).start()
        da = dot(gf[rows, :], w2[cols, :], 1, 1)
        du = (da * ring[lax.rem(m, RING)]).astype(BF16)
        acc[slot] += dot(du, w1[own_cols, cols], 1, 1)
        return rows, du

    def part_copy(i, out):
        far, near, sem = part_hbm.at[lax.rem(i, CHUNKS)], acc.at[lax.rem(i, SLOTS)], acc_sem.at[lax.rem(i, SLOTS)]
        return pltpu.make_async_copy(near, far, sem) if out else pltpu.make_async_copy(far, near, sem)

    def dw1_row(b):
        cols = pl.ds(al(b * f, f), f)
        return remote(dw1.at[pl.ds(al((1 - r) * half, half), half), cols], dw2t.at[:, cols], row_send.at[1 + b], row_recv.at[1 + b], sibling)

    def dw1_dep(b):
        cols = pl.ds(al(b * f, f), f)
        return remote(dw1.at[pl.ds(al(r * half + (1 - d) * q, q), q), cols], dw2t.at[0:q, pl.ds(al(hcols + b * f, f), f)], dep_send.at[1 + b], dep_recv.at[1 + b], layer)

    def dw1_out(b):
        cols = pl.ds(al(b * f, f), f)
        return pltpu.make_async_copy(dw1.at[pl.ds(al(r * half + d * q, q), q), cols], dw1_own.at[:, cols], own_sem.at[1 + b])

    def dw1_pass_on(b):
        cols = pl.ds(al(b * f, f), f)
        dw1_row(b).wait_recv()
        dw1[pl.ds(al(r * half, half), half), cols] += dw2t[:, cols]
        dw1_dep(b).start()

    @pl.loop(0, CHUNKS)
    def _(i):
        slot = lax.rem(i, SLOTS)

        @pl.when(i >= SLOTS)
        def _():
            part_copy(i, True).wait()
        act_copy(1, i).wait_recv()

        @pl.when(i < CHUNKS - AHEAD)
        def _():
            act_copy(1, i + AHEAD).start()

        @pl.when(i == CHUNKS - AHEAD)
        def _():
            w_copy(1, 6).start()
            w_copy(1, 8).start()

        @pl.when(i == CHUNKS - 2)
        def _():
            dw2_dep().wait()
            dw2t[:, dw2_mine] += dw2t[:, dw2_landing]
            dw2_out().start()

        @pl.when(i == CHUNKS - 1)
        def _():
            dw2_out().wait()
            for peer in (sibling, layer):
                pl.semaphore_signal(free_sem, inc=1, device_id=peer, device_id_type=MESH)

        acc[slot] = jnp.zeros_like(acc[slot])

        @pl.loop(0, hf)
        def _(jj):
            rows, du = backward(i, jj, i * hf + jj, slot)
            dw1[:, pl.ds(al(jj * f, f), f)] += dot(xf[rows, :], du, 0, 0)

            @pl.when(i == CHUNKS - 1)
            def _():
                @pl.when(jj == 0)
                def _():
                    pl.semaphore_wait(free_sem, 2)
                dw1_row(jj).start()

                @pl.when(jj >= 2)
                def _():
                    dw1_pass_on(jj - 2)

        part_copy(i, True).start()

    for b in range(hf - 2, hf):
        dw1_pass_on(b)
    for i in (0, 1):
        part_copy(i, True).wait()
        part_copy(i, False).start()
    w_copy(1, 6).wait_recv()
    w_copy(1, 7).start()
    w_copy(1, 7).wait_recv()

    @pl.loop(0, 2 * CHUNKS)
    def _(k):
        last = k // CHUNKS
        i = lax.rem(k, CHUNKS)
        slot = lax.rem(k, SLOTS)
        part_copy(k, False).wait()

        @pl.when(k < CHUNKS + 2)
        def _():
            part_copy(k + 2, True).wait()

        @pl.when(k < 2 * CHUNKS - 2)
        def _():
            part_copy(k + 2, False).start()

        @pl.when(k == CHUNKS)
        def _():
            w_copy(1, 8).wait_recv()
            w_copy(1, 9).start()
            w_copy(1, 9).wait_recv()

        @pl.loop(0, 2)
        def _(b):
            backward(i, hf + 2 * last + b, CHUNKS * hf + 2 * k + b, slot)

        @pl.when(last == 0)
        def _():
            part_copy(k, True).start()

        @pl.when(last == 1)
        def _():
            @pl.when(i >= 1)
            def _():
                put(dx_hbm, i).wait()
            out_buf[...] = acc[slot].astype(BF16)
            put(dx_hbm, i).start()

    for what in (0, 1, 2, 3, 4):
        for k in range(2):
            w_copy(k, what).wait_send()
    for what in (6, 7, 8, 9):
        w_copy(1, what).wait_send()
    for k in range(2):
        for i in range(CHUNKS):
            act_copy(k, i).wait_send()
    put(dx_hbm, 0).wait()
    for b in range(hf):
        dw1_dep(b).wait_recv()
        dw1[pl.ds(al(r * half + d * q, q), q), b * f:(b + 1) * f] += dw2t[0:q, hcols + b * f:hcols + (b + 1) * f]
        dw1_out(b).start()
    for b in range(hf):
        dw1_row(b).wait_send()
        dw1_dep(b).wait_send()
        dw1_out(b).wait()


def finish_kernel(y_in, dx_in, dw1_in, dw2_in, y_out, dx_out, dw1_out, dw2_out, y, dx, dw1, dw2t, dw2, in_sem, out_sem):
    copies = []
    for src, buf, dst, n in ((dw2_in, dw2t, None, PIECES), (y_in, y, y_out, PIECES), (dx_in, dx, dx_out, PIECES), (dw1_in, dw1, dw1_out, PIECES // 2)):
        rows = src.shape[0] // n
        for p in range(n):
            sl = pl.ds(p * rows, rows)
            copies.append((src.at[sl, :], buf.at[sl, :], None if dst is None else dst.at[sl, :]))
    ins = [pltpu.make_async_copy(a, b, in_sem.at[k]) for k, (a, b, _) in enumerate(copies)]
    for cp in ins:
        cp.start()
    outs = []
    for k, (_, b, o) in enumerate(copies):
        ins[k].wait()
        if o is None:
            rows = dw2t.shape[0] // PIECES
            dw2[:, k * rows:(k + 1) * rows] = dw2t[k * rows:(k + 1) * rows, :].T
            if k == PIECES - 1:
                outs.append(pltpu.make_async_copy(dw2, dw2_out, out_sem.at[k]))
                outs[-1].start()
        else:
            outs.append(pltpu.make_async_copy(b, o, out_sem.at[k]))
            outs[-1].start()
    for cp in outs:
        cp.wait()


def finish(y, dx, dw1, dw2t):
    sds = jax.ShapeDtypeStruct
    n = 3 * PIECES + PIECES // 2
    return pl.pallas_call(
        finish_kernel,
        out_shape=[sds(y.shape, BF16), sds(dx.shape, BF16), sds(dw1.shape, F32), sds(dw2t.shape[::-1], F32)],
        in_specs=[pl.BlockSpec(memory_space=pl.ANY)] * 4,
        out_specs=[pl.BlockSpec(memory_space=pl.ANY)] * 4,
        scratch_shapes=[
            pltpu.VMEM(y.shape, BF16), pltpu.VMEM(dx.shape, BF16), pltpu.VMEM(dw1.shape, F32),
            pltpu.VMEM(dw2t.shape, F32), pltpu.VMEM(dw2t.shape[::-1], F32),
            pltpu.SemaphoreType.DMA((n,)), pltpu.SemaphoreType.DMA((n,)),
        ],
        compiler_params=pltpu.CompilerParams(vmem_limit_bytes=60 * 1024 * 1024),
        name="finish",
    )(y, dx, dw1, dw2t)


def solution(mesh):
    act_spec = P(("dep", "row"), "col")
    wgt_spec = P("row", "col")
    grad_spec = P(("row", "dep"), "col")

    def local_block(x, w1, w2, g):
        tokens, half = x.shape
        hidden, hcols = w1.shape[0] * 2, w1.shape[1]
        ffn = hcols * 2
        t, f = tokens // CHUNKS, ffn // BLOCKS
        sds = jax.ShapeDtypeStruct
        dma = pltpu.SemaphoreType.DMA
        outs = pl.pallas_call(
            kernel,
            out_shape=[
                sds((tokens, half), BF16), sds((tokens, half), BF16),
                sds((half // 2, hcols), F32),
                sds((half, ffn // 4), F32),
                sds((CHUNKS, BLOCKS, t, f), F32), sds((CHUNKS, t, half), F32),
            ],
            in_specs=[pl.BlockSpec(memory_space=pl.ANY)] * 4,
            out_specs=[pl.BlockSpec(memory_space=pl.ANY)] * 6,
            scratch_shapes=[
                pltpu.VMEM((hidden, ffn), BF16), pltpu.VMEM((ffn, hidden), BF16),
                pltpu.VMEM((tokens, hidden), BF16), pltpu.VMEM((tokens, hidden), BF16),
                pltpu.VMEM((hidden, hcols), F32), pltpu.VMEM((half, ffn), F32),
                pltpu.VMEM((RING, t, f), F32), pltpu.VMEM((SLOTS, t, half), F32), pltpu.VMEM((t, half), BF16),
                dma((4,)), dma((2, 10)), dma((2, 10)), dma((2, CHUNKS)), dma((2, CHUNKS)),
                dma((RING,)), dma((SLOTS,)), dma((1,)),
                dma((1 + BLOCKS // 2,)), dma((1 + BLOCKS // 2,)), dma((1 + BLOCKS // 2,)), dma((1 + BLOCKS // 2,)), dma((1 + BLOCKS // 2,)),
                pltpu.SemaphoreType.REGULAR, pltpu.SemaphoreType.REGULAR,
            ],
            compiler_params=pltpu.CompilerParams(collective_id=0, has_side_effects=True, vmem_limit_bytes=67043328),
            name="mlp_block",
        )(x, w1, w2, g)
        return finish(*outs[:4])

    return jax.shard_map(local_block, mesh=mesh, in_specs=(act_spec, wgt_spec, wgt_spec, act_spec), out_specs=(act_spec, act_spec, grad_spec, grad_spec), check_vma=False)
```

time: 295 us -> 283 us (0.959)
  local copies, waits for them, and re-layouts: 8.48 us -> 0 us
  other arithmetic: 4.42 us -> 0 us
    pallas_call x0 -> x1, Pallas kernels: none -> 9.12 us  [finish(): pl.pallas_call(finish_kernel, out_shape=[sds(y.shape, BF16), sds(dx.shape...]
    pallas_call x1, Pallas kernels: 281 us -> 273 us  [local_block(): pl.pallas_call(kernel, out_shape=[sds((tokens, half), BF16), sds((tokens,...]
    unnamed x9 -> x0, local copies, waits for them, and re-layouts: 8.48 us -> none
    add x1 -> x0, other arithmetic: 4.03 us -> none  [local_block(): return (y, dx, dw1_own + dw1_got, (dw2_own + dw2_got).T)]
where the time goes in v3:
time: 283 us; the launch traced here: 282 us
  Pallas kernels  282 us (100%)
    pallas_call x1, Pallas kernels, local_block(): pl.pallas_call(kernel, out_shape=[sds((tokens, half), BF16), sds((tokens,...  273 us
    pallas_call x1, Pallas kernels, finish(): pl.pallas_call(finish_kernel, out_shape=[sds(y.shape, BF16), sds(dx.shape...  9.12 us

profile of v3, /device:TPU:0, one launch (start us, length us, event | category | flops | bytes accessed | tf_op | source)
XLA Modules:
  0.0 282.4 jit_solution(15835568445318277440)
XLA Ops:
  0.6 272.6 %mlp_block.1 = (bf16[4096,512]{1,0:T(8,128)(2,1)}, bf16[4096,512]{1,0:T(8,128)(2,1)}, f32[256,2048]{1,0:T(8,128)}, f32[512,1024]{1,0:T(8,128)}, f32[8,8,512,512]{3,2,1,0:T(8,128)}, /*index=5*/f32[8,512,512]{2,1,0:T(8,128)}) custom-call(bf16[4096,512]{1,0:T(8,128)(2,1)} %x_hbm.1, bf16[512,2048]{1,0:T(8,128)(2,1)} %w1_hbm.1, bf16[2048,512]{1,0:T(8,128)(2,1)} %w2_hbm.1, ...), custom_call_target="tpu_custom_call" | custom-call | tf_op jit(solution)/shard_map/mlp_block/pallas_call | solution.py:431
  273.3 9.1 %finish.1 = (bf16[4096,512]{1,0:T(8,128)(2,1)}, bf16[4096,512]{1,0:T(8,128)(2,1)}, f32[256,2048]{1,0:T(8,128)}, f32[1024,512]{1,0:T(8,128)}) custom-call(bf16[4096,512]{1,0:T(8,128)(2,1)} %get-tuple-element.8.y_in, bf16[4096,512]{1,0:T(8,128)(2,1)} %get-tuple-element.9.dx_in, f32[256,2048]{1,0:T(8,128)} %get-tuple-element.10.dw1_in, ...), custom_call_target="tpu_custom_call" | custom-call | tf_op jit(solution)/shard_map/finish/pallas_call | solution.py:404

commit v4 on v3

--- a/solution.py
+++ b/solution.py
@@ -31,9 +31,9 @@
     return lax.dot_general(a, b, (((ca,), (cb,)), ((), ())), preferred_element_type=F32)
 
 
-def kernel(x_hbm, w1_hbm, w2_hbm, g_hbm, y_hbm, dx_hbm, dw1_own, dw2_own, slope_hbm, part_hbm,
+def kernel(x_hbm, w1_hbm, w2_hbm, g_hbm, y_hbm, dx_hbm, dw1_own, dw2_own, give_hbm, slope_hbm, part_hbm,
            w1, w2, xf, gf, dw1, dw2t, ring, acc, out_buf,
-           load_sem, w_send, w_recv, x_send, x_recv, ring_sem, acc_sem, out_sem, row_send, row_recv, dep_send, dep_recv, own_sem, free_sem, room_sem):
+           load_sem, w_send, w_recv, x_send, x_recv, ring_sem, acc_sem, out_sem, row_send, row_recv, dep_send, dep_recv, own_sem, give_sem, free_sem, room_sem):
     d, c, r = lax.axis_index("dep"), lax.axis_index("col"), lax.axis_index("row")
     o = 1 - c
     across, layer, sibling = (d, o, r), (1 - d, c, r), (d, c, 1 - r)
@@ -43,6 +43,7 @@
     f = ffn // BLOCKS
     hf = BLOCKS // 2
     hcols, qcols, q = ffn // 2, ffn // 4, half // 2
+    e = f // 2
 
     barrier = pltpu.get_barrier_semaphore()
     for peer in (across, layer, sibling):
@@ -99,8 +100,7 @@
         return pltpu.make_async_copy(hbm, ref.at[:, pl.ds(al(c * half, half), half)], load_sem.at[2 + k])
 
     w_copy(0, 0).start()
-    for i in range(AHEAD):
-        act_copy(0, i).start()
+    act_copy(0, 0).start()
     for k in range(2):
         w_copy(k, 5).start()
         w_copy(k, 1).start()
@@ -110,6 +110,8 @@
     w_copy(0, 0).wait_recv()
     w_copy(0, 2).start()
     w_copy(0, 3).start()
+    for i in range(1, AHEAD):
+        act_copy(0, i).start()
     for k in range(2):
         w_copy(k, 5).wait()
         w_copy(k, 1).wait_recv()
@@ -226,10 +228,7 @@
         rows = pl.ds(al(i * t, t), t)
         cols = pl.ds(al(block_of(jj) * f, f), f)
         slope_in(m).wait()
-
-        @pl.when(m + RING - 1 < CHUNKS * BLOCKS)
-        def _():
-            slope_in(m + RING - 1).start()
+        slope_in(m + RING - 1).start()
         da = dot(gf[rows, :], w2[cols, :], 1, 1)
         du = (da * ring[lax.rem(m, RING)]).astype(BF16)
         acc[slot] += dot(du, w1[own_cols, cols], 1, 1)
@@ -243,19 +242,22 @@
         cols = pl.ds(al(b * f, f), f)
         return remote(dw1.at[pl.ds(al((1 - r) * half, half), half), cols], dw2t.at[:, cols], row_send.at[1 + b], row_recv.at[1 + b], sibling)
 
-    def dw1_dep(b):
-        cols = pl.ds(al(b * f, f), f)
-        return remote(dw1.at[pl.ds(al(r * half + (1 - d) * q, q), q), cols], dw2t.at[0:q, pl.ds(al(hcols + b * f, f), f)], dep_send.at[1 + b], dep_recv.at[1 + b], layer)
+    def dw1_dep(b, width=f):
+        src = dw1.at[pl.ds(al(r * half + (1 - d) * q, q), q), pl.ds(al(b * f, f), width)]
+        dst = dw2t.at[0:q, pl.ds(al(hcols + b * f, f), width)]
+        return remote(src, dst, dep_send.at[1 + b], dep_recv.at[1 + b], layer)
 
     def dw1_out(b):
         cols = pl.ds(al(b * f, f), f)
         return pltpu.make_async_copy(dw1.at[pl.ds(al(r * half + d * q, q), q), cols], dw1_own.at[:, cols], own_sem.at[1 + b])
 
-    def dw1_pass_on(b):
+    def dw1_take(b):
         cols = pl.ds(al(b * f, f), f)
         dw1_row(b).wait_recv()
         dw1[pl.ds(al(r * half, half), half), cols] += dw2t[:, cols]
-        dw1_dep(b).start()
+
+    def dw1_give():
+        return pltpu.make_async_copy(dw1.at[pl.ds(al(r * half + (1 - d) * q, q), q), pl.ds(hcols - e, e)], give_hbm, give_sem.at[0])
 
     @pl.loop(0, CHUNKS)
     def _(i):
@@ -303,15 +305,20 @@
 
                 @pl.when(jj >= 2)
                 def _():
-                    dw1_pass_on(jj - 2)
+                    dw1_take(jj - 2)
+                    dw1_dep(jj - 2).start()
 
         part_copy(i, True).start()
 
-    for b in range(hf - 2, hf):
-        dw1_pass_on(b)
+    dw1_take(hf - 2)
+    dw1_dep(hf - 2).start()
+    dw1_take(hf - 1)
+    dw1_dep(hf - 1, f - e).start()
+    dw1_give().start()
     for i in (0, 1):
         part_copy(i, True).wait()
         part_copy(i, False).start()
+    slope_in(CHUNKS * hf + RING - 1).start()
     w_copy(1, 6).wait_recv()
     w_copy(1, 7).start()
     w_copy(1, 7).wait_recv()
@@ -337,9 +344,20 @@
             w_copy(1, 9).start()
             w_copy(1, 9).wait_recv()
 
-        @pl.loop(0, 2)
-        def _(b):
-            backward(i, hf + 2 * last + b, CHUNKS * hf + 2 * k + b, slot)
+        m = CHUNKS * hf + 2 * k
+        slope_in(m).wait()
+        slope_in(m + 1).wait()
+        rows = pl.ds(al(i * t, t), t)
+        for b in range(2):
+            cols = pl.ds(al(block_of(hf + 2 * last + b) * f, f), f)
+            da = dot(gf[rows, :], w2[cols, :], 1, 1)
+            du = (da * ring[lax.rem(m + b, RING)]).astype(BF16)
+            acc[slot] += dot(du, w1[own_cols, cols], 1, 1)
+
+        @pl.when(k < 2 * CHUNKS - 2)
+        def _():
+            slope_in(m + 4).start()
+            slope_in(m + 5).start()
 
         @pl.when(last == 0)
         def _():
@@ -363,18 +381,20 @@
             act_copy(k, i).wait_send()
     put(dx_hbm, 0).wait()
     for b in range(hf):
-        dw1_dep(b).wait_recv()
-        dw1[pl.ds(al(r * half + d * q, q), q), b * f:(b + 1) * f] += dw2t[0:q, hcols + b * f:hcols + (b + 1) * f]
+        w = f if b < hf - 1 else f - e
+        dw1_dep(b, w).wait_recv()
+        dw1[pl.ds(al(r * half + d * q, q), q), b * f:b * f + w] += dw2t[0:q, hcols + b * f:hcols + b * f + w]
         dw1_out(b).start()
     for b in range(hf):
         dw1_row(b).wait_send()
-        dw1_dep(b).wait_send()
         dw1_out(b).wait()
+        dw1_dep(b, f if b < hf - 1 else f - e).wait_send()
+    dw1_give().wait()
 
 
 def finish_kernel(y_in, dx_in, dw1_in, dw2_in, y_out, dx_out, dw1_out, dw2_out, y, dx, dw1, dw2t, dw2, in_sem, out_sem):
     copies = []
-    for src, buf, dst, n in ((dw2_in, dw2t, None, PIECES), (y_in, y, y_out, PIECES), (dx_in, dx, dx_out, PIECES), (dw1_in, dw1, dw1_out, PIECES // 2)):
+    for src, buf, dst, n in ((y_in, y, y_out, PIECES), (dw2_in, dw2t, None, PIECES), (dx_in, dx, dx_out, PIECES), (dw1_in, dw1, dw1_out, PIECES // 2)):
         rows = src.shape[0] // n
         for p in range(n):
             sl = pl.ds(p * rows, rows)
@@ -387,8 +407,9 @@
         ins[k].wait()
         if o is None:
             rows = dw2t.shape[0] // PIECES
-            dw2[:, k * rows:(k + 1) * rows] = dw2t[k * rows:(k + 1) * rows, :].T
-            if k == PIECES - 1:
+            p = k - PIECES
+            dw2[:, p * rows:(p + 1) * rows] = dw2t[p * rows:(p + 1) * rows, :].T
+            if p == PIECES - 1:
                 outs.append(pltpu.make_async_copy(dw2, dw2_out, out_sem.at[k]))
                 outs[-1].start()
         else:
@@ -412,6 +433,7 @@
             pltpu.SemaphoreType.DMA((n,)), pltpu.SemaphoreType.DMA((n,)),
         ],
         compiler_params=pltpu.CompilerParams(vmem_limit_bytes=60 * 1024 * 1024),
+        cost_estimate=pl.CostEstimate(flops=2 * 10 ** 9, bytes_accessed=24 * 2 ** 20, transcendentals=0),
         name="finish",
     )(y, dx, dw1, dw2t)
 
@@ -434,10 +456,10 @@
                 sds((tokens, half), BF16), sds((tokens, half), BF16),
                 sds((half // 2, hcols), F32),
                 sds((half, ffn // 4), F32),
-                sds((CHUNKS, BLOCKS, t, f), F32), sds((CHUNKS, t, half), F32),
+                sds((half // 2, f // 2), F32), sds((CHUNKS, BLOCKS, t, f), F32), sds((CHUNKS, t, half), F32),
             ],
             in_specs=[pl.BlockSpec(memory_space=pl.ANY)] * 4,
-            out_specs=[pl.BlockSpec(memory_space=pl.ANY)] * 6,
+            out_specs=[pl.BlockSpec(memory_space=pl.ANY)] * 7,
             scratch_shapes=[
                 pltpu.VMEM((hidden, ffn), BF16), pltpu.VMEM((ffn, hidden), BF16),
                 pltpu.VMEM((tokens, hidden), BF16), pltpu.VMEM((tokens, hidden), BF16),
@@ -445,12 +467,14 @@
                 pltpu.VMEM((RING, t, f), F32), pltpu.VMEM((SLOTS, t, half), F32), pltpu.VMEM((t, half), BF16),
                 dma((4,)), dma((2, 10)), dma((2, 10)), dma((2, CHUNKS)), dma((2, CHUNKS)),
                 dma((RING,)), dma((SLOTS,)), dma((1,)),
-                dma((1 + BLOCKS // 2,)), dma((1 + BLOCKS // 2,)), dma((1 + BLOCKS // 2,)), dma((1 + BLOCKS // 2,)), dma((1 + BLOCKS // 2,)),
+                dma((1 + BLOCKS // 2,)), dma((1 + BLOCKS // 2,)), dma((1 + BLOCKS // 2,)), dma((1 + BLOCKS // 2,)), dma((1 + BLOCKS // 2,)), dma((1,)),
                 pltpu.SemaphoreType.REGULAR, pltpu.SemaphoreType.REGULAR,
             ],
             compiler_params=pltpu.CompilerParams(collective_id=0, has_side_effects=True, vmem_limit_bytes=67043328),
             name="mlp_block",
         )(x, w1, w2, g)
-        return finish(*outs[:4])
+        got = lax.ppermute(outs[4], "dep", [(0, 1), (1, 0)])
+        y, dx, dw1, dw2 = finish(*outs[:4])
+        return y, dx, dw1.at[:, hcols - f // 2:].add(got), dw2
 
     return jax.shard_map(local_block, mesh=mesh, in_specs=(act_spec, wgt_spec, wgt_spec, act_spec), out_specs=(act_spec, act_spec, grad_spec, grad_spec), check_vma=False)

time: 283 us -> 280 us (0.989)
  Pallas kernels: 282 us -> 277 us
    pallas_call x1, Pallas kernels: 273 us -> 268 us  [local_block(): pl.pallas_call(kernel, out_shape=[sds((tokens, half), BF16), sds((tokens,...]
  transfers between devices with their start and end apart: 0 -> 1, of which waited for: 0 -> 0; matrix products, arithmetic and copies ran while one was open for 0% -> 0% of each run, Pallas kernels for 0% -> 3%
where the time goes in v4:
time: 280 us
  Pallas kernels  277 us (99%)
    pallas_call x1, Pallas kernels, local_block(): pl.pallas_call(kernel, out_shape=[sds((tokens, half), BF16), sds((tokens,...  268 us
    pallas_call x1, Pallas kernels, finish(): pl.pallas_call(finish_kernel, out_shape=[sds(y.shape, BF16), sds(dx.shape...  9.02 us
  transfers between devices with their start and end apart: 1, of which 0 were waited for; matrix products, arithmetic and copies ran while one was open for 0% of the time, Pallas kernels for 3%

profile of v4, /device:TPU:0, one launch (start us, length us, event | category | flops | bytes accessed | tf_op | source)
XLA Modules:
  0.0 280.2 jit_solution(2064767942954267103)
XLA Ops:
  0.6 268.3 %mlp_block.1 = (bf16[4096,512]{1,0:T(8,128)(2,1)}, bf16[4096,512]{1,0:T(8,128)(2,1)}, f32[256,2048]{1,0:T(8,128)}, f32[512,1024]{1,0:T(8,128)}, f32[256,256]{1,0...) custom-call(bf16[4096,512]{1,0:T(8,128)(2,1)} %x_hbm.1, bf16[512,2048]{1,0:T(8,128)(2,1)} %w1_hbm.1, ...), custom_call_target="tpu_custom_call" | custom-call | tf_op jit(solution)/shard_map/mlp_block/pallas_call | solution.py:453
  268.9 0.6 collective-permute-start
  269.5 9.0 %finish.1 = (bf16[4096,512]{1,0:T(8,128)(2,1)}, bf16[4096,512]{1,0:T(8,128)(2,1)}, f32[256,2048]{1,0:T(8,128)}, f32[1024,512]{1,0:T(8,128)}) custom-call(bf16[4096,512]{1,0:T(8,128)(2,1)} %get-tuple-element.25.y_in, bf16[4096,512]{1,0:T(8,128)(2,1)} %get-tuple-element.26.dx_in, f32[256,2048]{1,0:T(8,128)} %get-tuple-element.27.dw1_in, ...), custom_call_target="tpu_custom_call" | custom-call | flops 2000000000 | bytes 25165824 | tf_op jit(solution)/shard_map/finish/pallas_call | solution.py:425
  278.5 0.0 collective-permute-done
  278.6 1.7 add_dynamic-update-slice_fusion
Async XLA Ops:
  268.9 9.6 %collective-permute-start = (f32[256,256]{1,0:T(8,128)}, f32[256,256]{1,0:T(8,128)S(1)}, u32[]{:S(2)}, u32[]{:S(2)}) collective-permute-start(f32[256,256]{1,0:T(8,128)} %get-tuple-element.32), channel_id=1, source_target_pairs={{0,4},{4,0},{1,5},{5,1},{2,6},{6,2},{3,7},{7,3}} | collective-permute-start | bytes 786440 | tf_op jit(solution)/shard_map/ppermute | solution.py:476

commit v5 on v4

--- a/solution.py
+++ b/solution.py
@@ -71,7 +71,9 @@
             return span((1 - col) * rows + dep * (rows // 2) + r * (rows // 4), rows // 4, col)
 
         def late(col):
-            return span(col * rows + (what // 8) * (rows // 2) + r * (rows // 4), rows // 4, col)
+            if what >= 10:
+                return span(col * rows + rows // 2 + r * (rows // 4), rows // 4, col)
+            return span(col * rows + (what // 8) * (rows // 4) + r * (rows // 8), rows // 8, col)
 
         block = span(r * rows, rows, c)
         if what == 5:
@@ -126,8 +128,10 @@
     def slope_in(m):
         first = CHUNKS * hf
         n = jnp.maximum(m - first, 0)
-        i = jnp.where(m < first, m // hf, lax.rem(n, first // 2) // 2)
-        jj = jnp.where(m < first, lax.rem(m, hf), hf + (n // (first // 2)) * 2 + lax.rem(n, 2))
+        i = jnp.where(n < 2 * SLOTS, lax.rem(n, SLOTS), lax.rem(n, first // 2) // 2)
+        jj = hf + jnp.where(n < 2 * SLOTS, n // SLOTS, (n // (first // 2)) * 2 + lax.rem(n, 2))
+        i = jnp.where(m < first, m // hf, i)
+        jj = jnp.where(m < first, lax.rem(m, hf), jj)
         slot = lax.rem(m, RING)
         return pltpu.make_async_copy(slope_hbm.at[i, jj], ring.at[slot], ring_sem.at[slot])
 
@@ -238,9 +242,12 @@
         far, near, sem = part_hbm.at[lax.rem(i, CHUNKS)], acc.at[lax.rem(i, SLOTS)], acc_sem.at[lax.rem(i, SLOTS)]
         return pltpu.make_async_copy(near, far, sem) if out else pltpu.make_async_copy(far, near, sem)
 
-    def dw1_row(b):
+    def dw1_row(b, own):
         cols = pl.ds(al(b * f, f), f)
-        return remote(dw1.at[pl.ds(al((1 - r) * half, half), half), cols], dw2t.at[:, cols], row_send.at[1 + b], row_recv.at[1 + b], sibling)
+        part = q * lax.rem(own + 1 + d, 2)
+        src = dw1.at[pl.ds(al((1 - r) * half + part, q), q), cols]
+        n = 1 + b + own * hf
+        return remote(src, dw2t.at[pl.ds(al(part, q), q), cols], row_send.at[n], row_recv.at[n], sibling)
 
     def dw1_dep(b, width=f):
         src = dw1.at[pl.ds(al(r * half + (1 - d) * q, q), q), pl.ds(al(b * f, f), width)]
@@ -251,10 +258,11 @@
         cols = pl.ds(al(b * f, f), f)
         return pltpu.make_async_copy(dw1.at[pl.ds(al(r * half + d * q, q), q), cols], dw1_own.at[:, cols], own_sem.at[1 + b])
 
-    def dw1_take(b):
+    def dw1_take(b, own):
         cols = pl.ds(al(b * f, f), f)
-        dw1_row(b).wait_recv()
-        dw1[pl.ds(al(r * half, half), half), cols] += dw2t[:, cols]
+        part = q * lax.rem(own + 1 + d, 2)
+        dw1_row(b, own).wait_recv()
+        dw1[pl.ds(al(r * half + part, q), q), cols] += dw2t[pl.ds(al(part, q), q), cols]
 
     def dw1_give():
         return pltpu.make_async_copy(dw1.at[pl.ds(al(r * half + (1 - d) * q, q), q), pl.ds(hcols - e, e)], give_hbm, give_sem.at[0])
@@ -276,6 +284,7 @@
         def _():
             w_copy(1, 6).start()
             w_copy(1, 8).start()
+            w_copy(1, 10).start()
 
         @pl.when(i == CHUNKS - 2)
         def _():
@@ -301,29 +310,63 @@
                 @pl.when(jj == 0)
                 def _():
                     pl.semaphore_wait(free_sem, 2)
-                dw1_row(jj).start()
-
-                @pl.when(jj >= 2)
+                dw1_row(jj, 0).start()
+                dw1_row(jj, 1).start()
+
+                @pl.when(lax.rem(jj, 2) == 1)
                 def _():
-                    dw1_take(jj - 2)
-                    dw1_dep(jj - 2).start()
+                    dw1_take(jj // 2, 0)
+                    dw1_dep(jj // 2).start()
 
         part_copy(i, True).start()
 
-    dw1_take(hf - 2)
-    dw1_dep(hf - 2).start()
-    dw1_take(hf - 1)
-    dw1_dep(hf - 1, f - e).start()
+    for b in range(hf // 2, hf):
+        dw1_take(b, 0)
+        dw1_dep(b, f if b < hf - 1 else f - e).start()
     dw1_give().start()
-    for i in (0, 1):
+    for b in range(hf):
+        dw1_take(b, 1)
+    for i in range(SLOTS):
         part_copy(i, True).wait()
         part_copy(i, False).start()
     slope_in(CHUNKS * hf + RING - 1).start()
-    w_copy(1, 6).wait_recv()
-    w_copy(1, 7).start()
-    w_copy(1, 7).wait_recv()
-
-    @pl.loop(0, 2 * CHUNKS)
+
+    def late_piece(what):
+        w_copy(1, what).wait_recv()
+        w_copy(1, what + 1).start()
+        w_copy(1, what + 1).wait_recv()
+
+    def second_pass(i, jj, count, m, slot):
+        for b in range(count):
+            slope_in(m + b).wait()
+        rows = pl.ds(al(i * t, t), t)
+        for b in range(count):
+            cols = pl.ds(al(block_of(jj + b) * f, f), f)
+            da = dot(gf[rows, :], w2[cols, :], 1, 1)
+            du = (da * ring[lax.rem(m + b, RING)]).astype(BF16)
+            acc[slot] += dot(du, w1[own_cols, cols], 1, 1)
+
+    late_piece(6)
+
+    @pl.loop(0, SLOTS)
+    def _(k):
+        part_copy(k, False).wait()
+        second_pass(k, hf, 1, CHUNKS * hf + k, k)
+        slope_in(CHUNKS * hf + k + RING).start()
+
+    late_piece(8)
+
+    @pl.loop(0, SLOTS)
+    def _(k):
+        @pl.when(k >= 2)
+        def _():
+            part_copy(k + 2, True).wait()
+            part_copy(k + 2, False).start()
+        second_pass(k, hf + 1, 1, CHUNKS * hf + SLOTS + k, k)
+        slope_in(CHUNKS * hf + SLOTS + k + RING).start()
+        part_copy(k, True).start()
+
+    @pl.loop(SLOTS, 2 * CHUNKS)
     def _(k):
         last = k // CHUNKS
         i = lax.rem(k, CHUNKS)
@@ -340,19 +383,10 @@
 
         @pl.when(k == CHUNKS)
         def _():
-            w_copy(1, 8).wait_recv()
-            w_copy(1, 9).start()
-            w_copy(1, 9).wait_recv()
+            late_piece(10)
 
         m = CHUNKS * hf + 2 * k
-        slope_in(m).wait()
-        slope_in(m + 1).wait()
-        rows = pl.ds(al(i * t, t), t)
-        for b in range(2):
-            cols = pl.ds(al(block_of(hf + 2 * last + b) * f, f), f)
-            da = dot(gf[rows, :], w2[cols, :], 1, 1)
-            du = (da * ring[lax.rem(m + b, RING)]).astype(BF16)
-            acc[slot] += dot(du, w1[own_cols, cols], 1, 1)
+        second_pass(i, hf + 2 * last, 2, m, slot)
 
         @pl.when(k < 2 * CHUNKS - 2)
         def _():
@@ -374,7 +408,7 @@
     for what in (0, 1, 2, 3, 4):
         for k in range(2):
             w_copy(k, what).wait_send()
-    for what in (6, 7, 8, 9):
+    for what in range(6, 12):
         w_copy(1, what).wait_send()
     for k in range(2):
         for i in range(CHUNKS):
@@ -386,7 +420,8 @@
         dw1[pl.ds(al(r * half + d * q, q), q), b * f:b * f + w] += dw2t[0:q, hcols + b * f:hcols + b * f + w]
         dw1_out(b).start()
     for b in range(hf):
-        dw1_row(b).wait_send()
+        dw1_row(b, 0).wait_send()
+        dw1_row(b, 1).wait_send()
         dw1_out(b).wait()
         dw1_dep(b, f if b < hf - 1 else f - e).wait_send()
     dw1_give().wait()
@@ -465,9 +500,9 @@
                 pltpu.VMEM((tokens, hidden), BF16), pltpu.VMEM((tokens, hidden), BF16),
                 pltpu.VMEM((hidden, hcols), F32), pltpu.VMEM((half, ffn), F32),
                 pltpu.VMEM((RING, t, f), F32), pltpu.VMEM((SLOTS, t, half), F32), pltpu.VMEM((t, half), BF16),
-                dma((4,)), dma((2, 10)), dma((2, 10)), dma((2, CHUNKS)), dma((2, CHUNKS)),
+                dma((4,)), dma((2, 12)), dma((2, 12)), dma((2, CHUNKS)), dma((2, CHUNKS)),
                 dma((RING,)), dma((SLOTS,)), dma((1,)),
-                dma((1 + BLOCKS // 2,)), dma((1 + BLOCKS // 2,)), dma((1 + BLOCKS // 2,)), dma((1 + BLOCKS // 2,)), dma((1 + BLOCKS // 2,)), dma((1,)),
+                dma((1 + BLOCKS,)), dma((1 + BLOCKS,)), dma((1 + BLOCKS // 2,)), dma((1 + BLOCKS // 2,)), dma((1 + BLOCKS // 2,)), dma((1,)),
                 pltpu.SemaphoreType.REGULAR, pltpu.SemaphoreType.REGULAR,
             ],
             compiler_params=pltpu.CompilerParams(collective_id=0, has_side_effects=True, vmem_limit_bytes=67043328),

time: 280 us -> 280 us (level)
  no operation moved by 1% of the time
where the time goes in v5:
time: 280 us
  Pallas kernels  277 us (99%)
    pallas_call x1, Pallas kernels, local_block(): pl.pallas_call(kernel, out_shape=[sds((tokens, half), BF16), sds((tokens,...  268 us
    pallas_call x1, Pallas kernels, finish(): pl.pallas_call(finish_kernel, out_shape=[sds(y.shape, BF16), sds(dx.shape...  9.02 us
  transfers between devices with their start and end apart: 1, of which 0 were waited for; matrix products, arithmetic and copies ran while one was open for 0% of the time, Pallas kernels for 3%

profile of v5, /device:TPU:0, one launch (start us, length us, event | category | flops | bytes accessed | tf_op | source)
XLA Modules:
  0.0 280.2 jit_solution(11160751251877464511)
XLA Ops:
  0.6 268.2 %mlp_block.1 = (bf16[4096,512]{1,0:T(8,128)(2,1)}, bf16[4096,512]{1,0:T(8,128)(2,1)}, f32[256,2048]{1,0:T(8,128)}, f32[512,1024]{1,0:T(8,128)}, f32[256,256]{1,0...) custom-call(bf16[4096,512]{1,0:T(8,128)(2,1)} %x_hbm.1, bf16[512,2048]{1,0:T(8,128)(2,1)} %w1_hbm.1, ...), custom_call_target="tpu_custom_call" | custom-call | tf_op jit(solution)/shard_map/mlp_block/pallas_call | solution.py:488
  268.9 0.6 collective-permute-start
  269.4 9.0 %finish.1 = (bf16[4096,512]{1,0:T(8,128)(2,1)}, bf16[4096,512]{1,0:T(8,128)(2,1)}, f32[256,2048]{1,0:T(8,128)}, f32[1024,512]{1,0:T(8,128)}) custom-call(bf16[4096,512]{1,0:T(8,128)(2,1)} %get-tuple-element.25.y_in, bf16[4096,512]{1,0:T(8,128)(2,1)} %get-tuple-element.26.dx_in, f32[256,2048]{1,0:T(8,128)} %get-tuple-element.27.dw1_in, ...), custom_call_target="tpu_custom_call" | custom-call | flops 2000000000 | bytes 25165824 | tf_op jit(solution)/shard_map/finish/pallas_call | solution.py:460
  278.5 0.0 collective-permute-done
  278.5 1.7 add_dynamic-update-slice_fusion
Async XLA Ops:
  268.9 9.6 %collective-permute-start = (f32[256,256]{1,0:T(8,128)}, f32[256,256]{1,0:T(8,128)S(1)}, u32[]{:S(2)}, u32[]{:S(2)}) collective-permute-start(f32[256,256]{1,0:T(8,128)} %get-tuple-element.32), channel_id=1, source_target_pairs={{0,4},{4,0},{1,5},{5,1},{2,6},{6,2},{3,7},{7,3}} | collective-permute-start | bytes 786440 | tf_op jit(solution)/shard_map/ppermute | solution.py:511
